TPU v7x, 8 devices: a whole 2x2x1 slice. The times are simulated.
8 devices in a mesh: data: 8 (over z, y, x, core).
Axes of the slice: x: 2, y: 2, z: 1, core: 2. Of those that a mesh axis runs over, the one named last changes fastest.
Arguments:
- h_a: bfloat16 [4096, 384], P('data')
- h_b: bfloat16 [4096, 384], P('data')
- w_one: bfloat16 [384, 2048], replicated
- w_two: bfloat16 [2048, 2048], replicated
- w_three: bfloat16 [2048, 2048], replicated
- gain_one: float32 [2048], replicated
- shift_one: float32 [2048], replicated
- gain_two: float32 [2048], replicated
- shift_two: float32 [2048], replicated
- lam_off: float32 [], replicated
Outputs:
- output 1: float32 [], replicated
- output 2: float32 [384, 2048], P('data')
- output 3: float32 [2048, 2048], P('data')
- output 4: float32 [2048, 2048], P('data')
- output 5: float32 [2048], replicated
- output 6: float32 [2048], replicated
- output 7: float32 [2048], replicated
- output 8: float32 [2048], replicated
All inputs are finite; a program needn't handle non-finite values.
Results may differ from a plain program's by a relative error of at most 0.00504015.
Values are sent between devices in bfloat16 or wider.
A program may use at most 1 GiB of HBM per device.

v0:
```python
import jax
import jax.numpy as jnp
from jax import lax
from jax.sharding import PartitionSpec as P

NORM_EPS = 1e-5
ROW_DIMS = (((0, 1), (0, 1)), ((), ()))
FIRST_DIMS = (((0,), (0,)), ((), ()))
LAST_DIMS = (((2,), (1,)), ((), ()))


def norm_forward(values, total_rows):
    col_sums = jnp.stack([jnp.sum(values, axis=1), jnp.sum(values * values, axis=1)])
    col_sums = lax.psum(col_sums, "data")
    col_mean = col_sums[0] / total_rows
    inv_std = lax.rsqrt(col_sums[1] / total_rows - col_mean * col_mean + NORM_EPS)
    return (values - col_mean[:, None, :]) * inv_std[:, None, :], inv_std


def norm_backward(grad_out, normed, inv_std, total_rows):
    col_sums = lax.psum(jnp.stack([jnp.sum(grad_out, axis=1), jnp.sum(grad_out * normed, axis=1)]), "data")
    grad_in = inv_std[:, None, :] * (grad_out - (col_sums[0][:, None, :] + normed * col_sums[1][:, None, :]) / total_rows)
    return grad_in, col_sums


def solution(mesh):
    shards = mesh.shape["data"]

    def local_step(h_a, h_b, w_one, w_two, w_three, gain_one, shift_one, gain_two, shift_two, lam_off):
        rows_dev = h_a.shape[0]
        total_rows = rows_dev * shards
        feat_rows = jnp.concatenate([h_a, h_b], axis=0)
        hidden_one = jnp.dot(feat_rows, w_one, preferred_element_type=jnp.float32).reshape(2, rows_dev, -1)
        normed_one, inv_one = norm_forward(hidden_one, total_rows)
        pre_one = gain_one * normed_one + shift_one
        act_one = jax.nn.relu(pre_one).astype(jnp.bfloat16)
        hidden_two = jnp.dot(act_one, w_two, preferred_element_type=jnp.float32)
        normed_two, inv_two = norm_forward(hidden_two, total_rows)
        pre_two = gain_two * normed_two + shift_two
        act_two = jax.nn.relu(pre_two).astype(jnp.bfloat16)
        proj_out = jnp.dot(act_two, w_three, preferred_element_type=jnp.float32)
        normed_out, inv_out = norm_forward(proj_out, total_rows)
        embed_pair = normed_out.astype(jnp.bfloat16)
        corr_part = lax.dot_general(embed_pair[0], embed_pair[1], FIRST_DIMS, preferred_element_type=jnp.float32)
        corr_mat = lax.psum(corr_part, "data") / total_rows
        feat_index = jnp.arange(corr_mat.shape[0])
        diag_mask = feat_index[:, None] == feat_index[None, :]
        diag_gap = 1.0 - corr_mat
        loss_total = jnp.sum(jnp.where(diag_mask, diag_gap * diag_gap, lam_off * corr_mat * corr_mat))
        grad_corr = jnp.where(diag_mask, -2.0 * diag_gap, 2.0 * lam_off * corr_mat)
        grad_scaled = (grad_corr / total_rows).astype(jnp.bfloat16)
        grad_embed_a = lax.dot_general(embed_pair[1], grad_scaled, (((1,), (1,)), ((), ())),
                                       preferred_element_type=jnp.float32)
        grad_embed_b = jnp.dot(embed_pair[0], grad_scaled, preferred_element_type=jnp.float32)
        grad_embed = jnp.stack([grad_embed_a, grad_embed_b])
        grad_proj = norm_backward(grad_embed, normed_out, inv_out, total_rows)[0].astype(jnp.bfloat16)
        grad_w_three = lax.psum_scatter(
            lax.dot_general(act_two, grad_proj, ROW_DIMS, preferred_element_type=jnp.float32),
            "data", scatter_dimension=0, tiled=True)
        grad_act_two = lax.dot_general(grad_proj, w_three, LAST_DIMS, preferred_element_type=jnp.float32)
        grad_pre_two = jnp.where(pre_two > 0, grad_act_two, 0.0)
        grad_hidden_two, sums_two = norm_backward(grad_pre_two, normed_two, inv_two, total_rows)
        grad_hidden_two = (gain_two * grad_hidden_two).astype(jnp.bfloat16)
        grad_w_two = lax.psum_scatter(
            lax.dot_general(act_one, grad_hidden_two, ROW_DIMS, preferred_element_type=jnp.float32),
            "data", scatter_dimension=0, tiled=True)
        grad_act_one = lax.dot_general(grad_hidden_two, w_two, LAST_DIMS, preferred_element_type=jnp.float32)
        grad_pre_one = jnp.where(pre_one > 0, grad_act_one, 0.0)
        grad_hidden_one, sums_one = norm_backward(grad_pre_one, normed_one, inv_one, total_rows)
        grad_hidden_one = (gain_one * grad_hidden_one).astype(jnp.bfloat16).reshape(2 * rows_dev, -1)
        grad_w_one = lax.psum_scatter(
            lax.dot_general(feat_rows, grad_hidden_one, FIRST_DIMS, preferred_element_type=jnp.float32),
            "data", scatter_dimension=0, tiled=True)
        return (loss_total, grad_w_one, grad_w_two, grad_w_three,
                jnp.sum(sums_one[1], axis=0), jnp.sum(sums_one[0], axis=0),
                jnp.sum(sums_two[1], axis=0), jnp.sum(sums_two[0], axis=0))

    row_spec = P("data", None)
    whole_mat = P(None, None)
    whole_vec = P(None)
    return jax.shard_map(
        local_step, mesh=mesh,
        in_specs=(row_spec, row_spec, whole_mat, whole_mat, whole_mat,
                  whole_vec, whole_vec, whole_vec, whole_vec, P()),
        out_specs=(P(), row_spec, row_spec, row_spec, whole_vec, whole_vec, whole_vec, whole_vec),
        check_vma=False)
```

profile of v0, /device:TPU:0, one launch (start us, length us, event | category | flops | bytes accessed | tf_op | source)
XLA Modules:
  0.0 778.7 jit_solution(17216662071564021310)
XLA Ops:
  7.2 0.0 copy-start
  7.2 0.0 copy-start.9
  7.2 0.0 copy-start.11
  7.2 0.0 all-reduce.2.cloned.1.call-start
  7.2 1.1 constant_dynamic-update-slice_fusion.1
  8.4 1.1 constant_dynamic-update-slice_fusion
  9.5 0.0 copy-start.6
  9.5 0.9 copy-done.6
  10.3 5.6 bitcast_reduce_fusion
  16.0 25.2 %psum.49 = f32[2,2,2048]{2,1,0:T(2,128)S(1)} all-reduce(f32[2,2,2048]{2,1,0:T(2,128)S(1)} %pad_maximum_fusion.1), channel_id=1, replica_groups=mesh['data'=8] {'data'}, use_global_device_ids=true, to_apply=%region_2.0 | all-reduce | flops 8192 | bytes 65536 | tf_op jit(solution)/shard_map/psum | solution.py:14
  41.3 0.0 copy-start.8
  41.3 0.0 copy-start.10
  41.3 15.8 %fusion.35 = (f32[2,2048]{1,0:T(2,128)S(1)}, f32[2,2048]{1,0:T(2,128)S(1)}, f32[2,512,2048]{2,1,0:T(8,128)}) fusion(bf16[2048,2048]{1,0:T(8,128)(2,1)} %param.13, f32[1024,2048]{1,0:T(8,128)} %get-tuple-element.30, f32[2048]{0:T(1024)S(1)} %copy-done.11, f32[2,2048]{1,0:T(2,128)S(1)} %fusion.30, f32[2,2048]{1,0:T(2,128)S(1)} %fusion.31, f32[2048]{0:T(1024)S(1)} %copy-done.9), kind=kOutput, calls=%fused_computation.84 | convolution fusion | flops 8608800768 | bytes 25247744 | tf_op jit(solution)/shard_map/dot_general | solution.py:37
  57.2 23.2 %psum.50 = f32[2,2,2048]{2,1,0:T(2,128)S(1)} all-reduce(f32[2,2,2048]{2,1,0:T(2,128)S(1)} %pad_maximum_fusion.2), channel_id=1, replica_groups=mesh['data'=8] {'data'}, use_global_device_ids=true, to_apply=%region_5.6 | all-reduce | flops 8192 | bytes 65536 | tf_op jit(solution)/shard_map/psum | solution.py:14
  80.4 15.8 %fusion.34 = (f32[2,2048]{1,0:T(2,128)S(1)}, f32[2,2048]{1,0:T(2,128)S(1)}, f32[2,512,2048]{2,1,0:T(8,128)}) fusion(bf16[2048,2048]{1,0:T(8,128)(2,1)} %param.14, f32[2,512,2048]{2,1,0:T(8,128)} %get-tuple-element.31, f32[2048]{0:T(1024)S(1)} %copy-done.10, f32[2,2048]{1,0:T(2,128)S(1)} %fusion.25, f32[2,2048]{1,0:T(2,128)S(1)} %fusion.26, ...), kind=kOutput, calls=%fused_computation.83 | convolution fusion | flops 8608800768 | bytes 25247744 | tf_op jit(solution)/shard_map/dot_general | solution.py:41
  96.2 24.4 %psum.51 = f32[2,2,2048]{2,1,0:T(2,128)S(1)} all-reduce(f32[2,2,2048]{2,1,0:T(2,128)S(1)} %pad_maximum_fusion.3), channel_id=1, replica_groups=mesh['data'=8] {'data'}, use_global_device_ids=true, to_apply=%region_8.9 | all-reduce | flops 8192 | bytes 65536 | tf_op jit(solution)/shard_map/psum | solution.py:14
  120.7 4.6 fusion.10
  125.3 1.9 copy-done.5
  127.2 8.1 %fusion.16 = f32[2048,2048]{1,0:T(8,128)} fusion(bf16[2,512,2048]{2,1,0:T(8,128)(2,1)S(1)} %fusion.10), kind=kOutput, calls=%fused_computation.41 | convolution fusion | flops 4294967296 | bytes 20971520 | tf_op jit(solution)/shard_map/dot_general | solution.py:44
  135.3 0.0 all-reduce.2.cloned.1.call-update
  135.3 0.0 reduce-scatter.4.cloned.1.call-start
  136.0 206.5 %all-reduce.2.cloned.1.call-done = f32[2048,2048]{1,0:T(8,128)} async-done(((f32[2048,2048]{1,0:T(8,128)}), f32[2048,2048]{1,0:T(8,128)}) %all-reduce.2.cloned.1.call-update) | async-done | bytes 16777232 | tf_op jit(solution)/shard_map/psum | solution.py:45
  342.5 12.4 %convolution_bitcast_fusion.3 = f32[1,512,2048]{2,1,0:T(8,128)} fusion(bf16[2,512,2048]{2,1,0:T(8,128)(2,1)} %copy-done.5, f32[2048,2048]{1,0:T(8,128)} %all-reduce.2.cloned.1.call-done, f32[]{:T(128)S(6)} %mul.190), kind=kOutput, calls=%fused_computation.38 | convolution fusion | flops 4328521728 | bytes 23068676 | tf_op jit(solution)/shard_map/dot_general | solution.py:52
  354.9 9.3 %convolution_bitcast_fusion.2 = f32[1,512,2048]{2,1,0:T(8,128)} fusion(bf16[2,512,2048]{2,1,0:T(8,128)(2,1)} %copy-done.5, f32[2048,2048]{1,0:T(8,128)S(1)} %copy-done.2, f32[]{:T(128)S(6)} %mul.190), kind=kOutput, calls=%fused_computation.37 | convolution fusion | flops 4328521728 | bytes 23068676 | tf_op jit(solution)/shard_map/dot_general | solution.py:54
  364.2 4.6 fusion.11
  368.8 33.3 %psum.53 = f32[2,2,2048]{2,1,0:T(2,128)S(1)} all-reduce(f32[2,2,2048]{2,1,0:T(2,128)S(1)} %pad_maximum_fusion.4), channel_id=1, replica_groups=mesh['data'=8] {'data'}, use_global_device_ids=true, to_apply=%region_13.14 | all-reduce | flops 8192 | bytes 65536 | tf_op jit(solution)/shard_map/psum | solution.py:21
  402.1 7.1 multiply_convert_fusion.3
  409.2 17.4 %fusion.33 = (f32[2,2048]{1,0:T(2,128)S(1)}, f32[2,2048]{1,0:T(2,128)S(1)}, f32[2,512,2048]{2,1,0:T(8,128)}) fusion(f32[2,2048]{1,0:T(2,128)S(1)} %fusion.25, f32[2,512,2048]{2,1,0:T(8,128)} %get-tuple-element.31, f32[2,2048]{1,0:T(2,128)S(1)} %fusion.26, bf16[2,512,2048]{2,1,0:T(8,128)(2,1)S(1)} %multiply_convert_fusion.3, bf16[2048,2048]{1,0:T(8,128)(2,1)} %param.14, ...), kind=kOutput, calls=%fused_computation.82 | convolution fusion | flops 8608800768 | bytes 29442048 | tf_op jit(solution)/shard_map/dot_general | solution.py:60
  426.6 24.1 %psum.54 = f32[2,2,2048]{2,1,0:T(2,128)S(1)} all-reduce(f32[2,2,2048]{2,1,0:T(2,128)S(1)} %pad_maximum_fusion.5), channel_id=1, replica_groups=mesh['data'=8] {'data'}, use_global_device_ids=true, to_apply=%region_16.17 | all-reduce | flops 8192 | bytes 65536 | tf_op jit(solution)/shard_map/psum | solution.py:21
  450.8 0.6 slice_reduce_fusion.3
  451.4 7.1 multiply_convert_fusion.2
  458.6 0.0 copy-start.4
  458.6 17.4 %fusion.32 = (f32[2,2048]{1,0:T(2,128)S(1)}, f32[2,2048]{1,0:T(2,128)S(1)}, f32[2,512,2048]{2,1,0:T(8,128)}) fusion(f32[2,2048]{1,0:T(2,128)S(1)} %fusion.30, f32[2,2048]{1,0:T(2,128)S(1)} %fusion.31, f32[1024,2048]{1,0:T(8,128)} %get-tuple-element.30, bf16[2,512,2048]{2,1,0:T(8,128)(2,1)S(1)} %multiply_convert_fusion.2, bf16[2048,2048]{1,0:T(8,128)(2,1)} %param.13, ...), kind=kOutput, calls=%fused_computation.81 | convolution fusion | flops 8608800768 | bytes 29442048 | tf_op jit(solution)/shard_map/dot_general | solution.py:67
  476.0 23.2 %psum.55 = f32[2,2,2048]{2,1,0:T(2,128)S(1)} all-reduce(f32[2,2,2048]{2,1,0:T(2,128)S(1)} %pad_maximum_fusion.6), channel_id=1, replica_groups=mesh['data'=8] {'data'}, use_global_device_ids=true, to_apply=%region_19.20 | all-reduce | flops 8192 | bytes 65536 | tf_op jit(solution)/shard_map/psum | solution.py:21
  499.2 0.6 slice_reduce_fusion.1
  499.8 7.1 multiply_convert_fusion.1
  507.0 3.5 fusion.36
  510.6 0.0 reduce-scatter.4.cloned.1.call-update
  510.6 0.3 reduce-scatter.8.cloned.1.call-start
  510.8 15.9 %convolution_bitcast_fusion = f32[2048,2048]{1,0:T(8,128)} fusion(bf16[2,512,2048]{2,1,0:T(8,128)(2,1)} %copy-done.3, f32[2,512,2048]{2,1,0:T(8,128)} %get-tuple-element.31, f32[2048]{0:T(1024)S(1)} %copy-done.10, f32[2,2048]{1,0:T(2,128)S(1)} %fusion.25, f32[2,2048]{1,0:T(2,128)S(1)} %fusion.26, f32[2048]{0:T(1024)S(1)} %copy-done.8), kind=kOutput, calls=%fused_computation.3 | convolution fusion | flops 8602517504 | bytes 29409280 | tf_op jit(solution)/shard_map/dot_general | solution.py:58
  526.7 0.0 reduce-scatter.8.cloned.1.call-update
  526.8 0.0 reduce-scatter.6.cloned.1.call-start
  526.8 15.9 %convolution_bitcast_fusion.1 = f32[2048,2048]{1,0:T(8,128)} fusion(bf16[2,512,2048]{2,1,0:T(8,128)(2,1)} %copy-done.4, f32[1024,2048]{1,0:T(8,128)} %get-tuple-element.30, f32[2048]{0:T(1024)S(1)} %copy-done.11, f32[2,2048]{1,0:T(2,128)S(1)} %fusion.30, f32[2,2048]{1,0:T(2,128)S(1)} %fusion.31, f32[2048]{0:T(1024)S(1)} %copy-done.9), kind=kOutput, calls=%fused_computation.4 | convolution fusion | flops 8602517504 | bytes 29409280 | tf_op jit(solution)/shard_map/dot_general | solution.py:65
  542.7 0.0 reduce-scatter.6.cloned.1.call-update
  542.7 0.0 copy-start.1
  542.7 8.9 %select_reduce_fusion = f32[]{:T(128)} fusion(f32[2048,2048]{1,0:T(8,128)} %all-reduce.2.cloned.1.call-done, f32[]{:T(128)S(6)} %mul.184), kind=kLoop, calls=%fused_computation.1 | loop fusion | flops 33554432 | bytes 16777224 | tf_op jit(solution)/shard_map/reduce_sum | solution.py:49
  551.6 109.4 %reduce-scatter.8.cloned.1.call-done = f32[256,2048]{1,0:T(8,128)} async-done(((f32[2048,2048]{1,0:T(8,128)}), f32[256,2048]{1,0:T(8,128)}) %reduce-scatter.8.cloned.1.call-update) | async-done | bytes 2097168 | tf_op jit(solution)/shard_map/reduce_scatter | solution.py:57
  661.0 110.9 %reduce-scatter.6.cloned.1.call-done = f32[256,2048]{1,0:T(8,128)} async-done(((f32[2048,2048]{1,0:T(8,128)}), f32[256,2048]{1,0:T(8,128)}) %reduce-scatter.6.cloned.1.call-update) | async-done | bytes 2097168 | tf_op jit(solution)/shard_map/reduce_scatter | solution.py:64
  (33 shorter events, 0.2 us)
Async XLA Ops:
  7.2 3.2 copy-start
  7.2 34.1 %copy-start.9 = (f32[2048]{0:T(1024)S(1)}, f32[2048]{0:T(1024)}, u32[]{:S(2)}) copy-start(f32[2048]{0:T(1024)} %param.15) | copy-start | bytes 24580
  7.2 34.1 %copy-start.11 = (f32[2048]{0:T(1024)S(1)}, f32[2048]{0:T(1024)}, u32[]{:S(2)}) copy-start(f32[2048]{0:T(1024)} %param.16) | copy-start | bytes 24580
  7.2 335.3 %all-reduce.2.cloned.1.call-start = ((), (), s32[]{:S(2)}) async-start(), calls=%async_computation.3 | async-start | bytes 33554432 | tf_op jit(solution)/shard_map/psum | solution.py:45
  9.5 0.9 copy-start.6
  41.3 39.1 %copy-start.8 = (f32[2048]{0:T(1024)S(1)}, f32[2048]{0:T(1024)}, u32[]{:S(2)}) copy-start(f32[2048]{0:T(1024)} %param.17) | copy-start | bytes 24580
  41.3 39.1 %copy-start.10 = (f32[2048]{0:T(1024)S(1)}, f32[2048]{0:T(1024)}, u32[]{:S(2)}) copy-start(f32[2048]{0:T(1024)} %param.18) | copy-start | bytes 24580
  125.3 1.9 copy-start.5
  135.3 416.3 %reduce-scatter.4.cloned.1.call-start = ((), (), s32[]{:S(2)}) async-start(), calls=%async_computation.4 | async-start | bytes 3538944 | tf_op jit(solution)/shard_map/reduce_scatter | solution.py:71
  342.5 12.4 %copy-start.2 = (f32[2048,2048]{1,0:T(8,128)S(1)}, f32[2048,2048]{1,0:T(8,128)}, u32[]{:S(2)}) copy-start(f32[2048,2048]{1,0:T(8,128)} %all-reduce.2.cloned.1.call-done) | copy-start | bytes 50331652
  342.5 21.7 %slice-start = ((s8[8388608]{0:T(1024)(128)(4,1)}), s8[4194304]{0:T(1024)(128)(4,1)S(1)}, s32[]{:S(2)}) async-start(s8[8388608]{0:T(1024)(128)(4,1)} %bitcast.127), calls=%async_computation.7 | async-start | bytes 8388608
  354.9 9.3 %slice-start.1 = ((s8[8388608]{0:T(1024)(128)(4,1)}), s8[4194304]{0:T(1024)(128)(4,1)S(1)}, s32[]{:S(2)}) async-start(s8[8388608]{0:T(1024)(128)(4,1)} %bitcast.127), calls=%async_computation.8 | async-start | bytes 8388608
  409.2 17.4 %copy-start.3 = (bf16[2,512,2048]{2,1,0:T(8,128)(2,1)}, bf16[2,512,2048]{2,1,0:T(8,128)(2,1)S(1)}, u32[]{:S(2)}) copy-start(bf16[2,512,2048]{2,1,0:T(8,128)(2,1)S(1)} %multiply_convert_fusion.3) | copy-start | bytes 12582916
  458.6 17.4 %copy-start.4 = (bf16[2,512,2048]{2,1,0:T(8,128)(2,1)}, bf16[2,512,2048]{2,1,0:T(8,128)(2,1)S(1)}, u32[]{:S(2)}) copy-start(bf16[2,512,2048]{2,1,0:T(8,128)(2,1)S(1)} %multiply_convert_fusion.2) | copy-start | bytes 12582916
  499.8 7.2 copy-start.7
  510.6 150.4 %reduce-scatter.8.cloned.1.call-start = ((), (), s32[]{:S(2)}) async-start(), calls=%async_computation.6 | async-start | bytes 18874368 | tf_op jit(solution)/shard_map/reduce_scatter | solution.py:57
  526.8 245.1 %reduce-scatter.6.cloned.1.call-start = ((), (), s32[]{:S(2)}) async-start(), calls=%async_computation.5 | async-start | bytes 18874368 | tf_op jit(solution)/shard_map/reduce_scatter | solution.py:64
  542.7 229.1 %copy-start.1 = (bf16[384,2048]{1,0:T(8,128)(2,1)S(1)}, bf16[384,2048]{1,0:T(8,128)(2,1)}, u32[]{:S(2)}) copy-start(bf16[384,2048]{1,0:T(8,128)(2,1)} %param.12) | copy-start | bytes 4718596
Sparse Core Ops, SparseCore 0:
  135.4 207.0 all-reduce.1
  510.7 39.2 reduce-scatter.3
  554.0 106.8 reduce-scatter.7
  664.9 106.9 reduce-scatter.5
where the time goes:
time: 788 us; the launch traced here: 779 us
  waiting for transfers between devices  427 us (54%)
  blocking collectives  153 us (19%)
  matrix products  137 us (17%)
  other arithmetic  40.9 us (5%)
  between operations  15.1 us (2%)
    psum x1, waiting for transfers between devices, local_step(): corr_mat = lax.psum(corr_part, 'data') / total_rows  206 us
    reduce_scatter x1, waiting for transfers between devices, local_step(): lax.psum_scatter(lax.dot_general(act_one, grad_hidden_two, ROW_DIMS, pref...  111 us
    reduce_scatter x1, waiting for transfers between devices, local_step(): lax.psum_scatter(lax.dot_general(act_two, grad_proj, ROW_DIMS, preferred_...  109 us
    psum x3, blocking collectives, norm_backward(): lax.psum(jnp.stack([jnp.sum(grad_out, axis=1), jnp.sum(grad_out * normed,...  80.6 us
    psum x3, blocking collectives, norm_forward(): col_sums = lax.psum(col_sums, 'data')  72.8 us
    dot_general x1, matrix products, local_step(): lax.dot_general(grad_proj, w_three, LAST_DIMS, preferred_element_type=jnp...  17.4 us
    dot_general x1, matrix products, local_step(): lax.dot_general(grad_hidden_two, w_two, LAST_DIMS, preferred_element_type...  17.4 us
    dot_general x1, matrix products, local_step(): lax.dot_general(act_two, grad_proj, ROW_DIMS, preferred_element_type=jnp....  15.9 us
  transfers between devices with their start and end apart: 4, of which 3 were waited for; matrix products, arithmetic and copies ran while one was open for 5% of the time, Pallas kernels for 0%

commit v1 on v0

v1 whole, which is shorter than its diff:
```python
import functools

import jax
import jax.numpy as jnp
from jax import lax
from jax.experimental import pallas as pl
from jax.experimental.pallas import tpu as pltpu
from jax.sharding import PartitionSpec as P

MESH = pl.DeviceIdType.MESH
F32, BF16 = jnp.float32, jnp.bfloat16
NORM_EPS = 1e-5
TOTAL_ROWS = 4096
VIEW = 512
ROWS = 2 * VIEW
FEAT = 384
WIDTH = 2048
TILE = 256
TILES = WIDTH // TILE
PIECE = FEAT // 8
LAG_C, LAG_D = 2, 4
PA_SLOTS, R0_SLOTS, R1_SLOTS, R2_SLOTS = 5, 2, 4, 4


def dot_nn(a, b):
    return jnp.dot(a, b, preferred_element_type=F32)


def dot_nt(a, b):
    return lax.dot_general(a, b, (((1,), (1,)), ((), ())), preferred_element_type=F32)


def when_in(cond, fn):
    if isinstance(cond, bool):
        if cond:
            fn()
    else:
        pl.when(cond)(fn)


def peer_of(me, r):
    out = me
    for bit in (1, 2, 4):
        if r & bit:
            out = out + bit - 2 * bit * ((me // bit) % 2)
    return out


def entry_barrier(me):
    barrier = pltpu.get_barrier_semaphore()
    for r in range(1, 8):
        pl.semaphore_signal(barrier, inc=1, device_id=(peer_of(me, r),), device_id_type=MESH)
    pl.semaphore_wait(barrier, 7)


def cols(t, width=TILE):
    if isinstance(t, int):
        return pl.ds(t * width, width)
    return pl.ds(pl.multiple_of(t * width, width), width)


def stats_send(me, st, ssem, rsem, i):
    for r in range(1, 8):
        pltpu.make_async_remote_copy(
            src_ref=st.at[i, 0], dst_ref=st.at[i, r], send_sem=ssem.at[i], recv_sem=rsem.at[i],
            device_id=(peer_of(me, r),), device_id_type=MESH).start()


def stats_wait(st, ssem, rsem, i):
    block = st.at[i, pl.ds(1, 7)]
    pltpu.make_async_copy(block, block, rsem.at[i]).wait()
    pltpu.make_async_copy(block, block, ssem.at[i]).wait()


def stats_total(st, i):
    pairs = [st[i, 2 * k] + st[i, 2 * k + 1] for k in range(4)]
    return (pairs[0] + pairs[1]) + (pairs[2] + pairs[3])


def stats_put(st, i, values, weighted):
    rows = []
    for v in range(2):
        part = slice(v * VIEW, (v + 1) * VIEW)
        rows.append(jnp.sum(values[part], axis=0, keepdims=True))
        rows.append(jnp.sum(weighted[part], axis=0, keepdims=True))
    for k in range(4):
        st[i, 0, pl.ds(k, 1), :] = rows[k]


def forward_kernel(h_a, h_b, w1_hbm, w2_hbm, w3_hbm, g1, b1, g2, b2,
                   x1, x2, zh, inv_out, xh1_hbm, xh2_hbm, zn_hbm,
                   w1, wb, u, st, w1_sem, w_sem, out_sem, ssem, rsem):
    me = lax.axis_index("data")
    w1_copy = pltpu.make_async_copy(w1_hbm, w1, w1_sem)
    w1_copy.start()

    def w_copy(layer, q):
        src = (w2_hbm, w3_hbm)[layer]
        return pltpu.make_async_copy(src.at[:, cols(q)], wb.at[layer, q], w_sem.at[layer, q])

    for layer in range(2):
        for q in range(TILES):
            w_copy(layer, q).start()
    entry_barrier(me)
    w1_copy.wait()

    outs_hbm = (xh1_hbm, xh2_hbm, zn_hbm)
    acts = (x1, x2, zh)

    def out_copy(layer, q):
        return pltpu.make_async_copy(u.at[q], outs_hbm[layer].at[q], out_sem.at[q])

    for layer in range(3):
        base = layer * TILES

        def matmul_tile(q, carry, layer=layer, base=base):
            if layer > 0:
                out_copy(layer - 1, q).wait()
                w_copy(layer - 1, q).wait()
                vals = dot_nn(acts[layer - 1][...], wb[layer - 1, q])
            else:
                tile = w1[:, cols(q)]
                vals = jnp.concatenate([dot_nn(h_a[...], tile), dot_nn(h_b[...], tile)], axis=0)
            u[q] = vals
            stats_put(st, base + q, vals, vals * vals)
            stats_send(me, st, ssem, rsem, base + q)
            return carry

        lax.fori_loop(0, TILES, matmul_tile, 0)

        def norm_tile(q, carry, layer=layer, base=base):
            stats_wait(st, ssem, rsem, base + q)
            total = stats_total(st, base + q) * (1.0 / TOTAL_ROWS)
            for v in range(2):
                mean = total[2 * v:2 * v + 1]
                inv = lax.rsqrt(total[2 * v + 1:2 * v + 2] - mean * mean + NORM_EPS)
                inv_out[layer, q, pl.ds(v, 1), :] = inv
                rows = pl.ds(v * VIEW, VIEW)
                normed = (u[q, rows, :] - mean) * inv
                u[q, rows, :] = normed
                if layer < 2:
                    gain, shift = ((g1, b1), (g2, b2))[layer]
                    normed = jnp.maximum(gain[:, cols(q)] * normed + shift[:, cols(q)], 0.0)
                acts[layer][rows, cols(q)] = normed.astype(BF16)
            out_copy(layer, q).start()
            return carry

        lax.fori_loop(0, TILES, norm_tile, 0)
    for q in range(TILES):
        out_copy(2, q).wait()


class Ring:
    def __init__(self, me, items, pa, r0, r1, r2, sems, credits):
        self.items, self.pa, self.r0, self.r1, self.r2 = items, pa, r0, r1, r2
        self.s0, self.q0, self.s1, self.q1, self.s2, self.q2 = sems
        self.c0, self.c1, self.c2 = credits
        core = me % 2
        x, y = (me // 2) % 2, me // 4
        self.core = core
        self.f = x + core * (y - x)
        self.s = y + core * (x - y)
        x_side, y_side = me + 2 - 4 * x, me + 4 - 8 * y
        self.partner = me + 1 - 2 * core
        self.first = x_side + core * (y_side - x_side)
        self.second = y_side + core * (x_side - y_side)

    def copy(self, src, dst, send, recv, device):
        return pltpu.make_async_remote_copy(src_ref=src, dst_ref=dst, send_sem=send, recv_sem=recv,
                                            device_id=(device,), device_id_type=MESH)

    def copy0(self, t, rows):
        return self.copy(self.pa.at[t % PA_SLOTS, 1 - self.core, :, :, pl.ds(0, rows)],
                         self.r0.at[t % R0_SLOTS, :, :, pl.ds(0, rows)],
                         self.s0.at[t % R0_SLOTS], self.q0.at[t % R0_SLOTS], self.partner)

    def copy1(self, t, rows):
        return self.copy(self.pa.at[t % PA_SLOTS, self.core, 1 - self.f, :, pl.ds(0, rows)],
                         self.r1.at[t % R1_SLOTS, :, pl.ds(0, rows)],
                         self.s1.at[t % R1_SLOTS], self.q1.at[t % R1_SLOTS], self.first)

    def copy2(self, t, rows):
        return self.copy(self.pa.at[t % PA_SLOTS, self.core, self.f, 1 - self.s, pl.ds(0, rows)],
                         self.r2.at[t % R2_SLOTS, pl.ds(0, rows)],
                         self.s2.at[t % R2_SLOTS], self.q2.at[t % R2_SLOTS], self.second)

    def take_credit(self, sem, t, slots):
        when_in(t >= slots, lambda: pl.semaphore_wait(sem, 1))

    def give_credit(self, sem, t, slots, device):
        when_in(t + slots < self.items,
                lambda: pl.semaphore_signal(sem, inc=1, device_id=(device,), device_id_type=MESH))

    def send0(self, t, rows=TILE):
        self.take_credit(self.c0, t, R0_SLOTS)
        self.copy0(t, rows).start()

    def stage_b(self, t, rows=TILE):
        self.copy0(t, rows).wait()
        slot = t % PA_SLOTS
        for k in range(4):
            a, b = k // 2, k % 2
            self.pa[slot, self.core, a, b, :rows] += self.r0[t % R0_SLOTS, a, b, :rows]
        self.give_credit(self.c0, t, R0_SLOTS, self.partner)
        self.take_credit(self.c1, t, R1_SLOTS)
        self.copy1(t, rows).start()

    def stage_c(self, t, rows=TILE):
        self.copy1(t, rows).wait()
        slot = t % PA_SLOTS
        for b in range(2):
            self.pa[slot, self.core, self.f, b, :rows] += self.r1[t % R1_SLOTS, b, :rows]
        self.give_credit(self.c1, t, R1_SLOTS, self.first)
        self.take_credit(self.c2, t, R2_SLOTS)
        self.copy2(t, rows).start()

    def stage_d(self, t, rows=TILE):
        self.copy2(t, rows).wait()
        total = self.pa[t % PA_SLOTS, self.core, self.f, self.s, :rows] + self.r2[t % R2_SLOTS, :rows]
        self.give_credit(self.c2, t, R2_SLOTS, self.second)
        return total

    def partial(self, t, lt, right):
        for half in range(2):
            core = self.core if half else 1 - self.core

            def block(k, carry, core=core):
                a, b = k // 2, k % 2
                dev = core + a * (2 + 2 * core) + b * (4 - 2 * core)
                self.pa[t % PA_SLOTS, core, a, b] = dot_nn(lt[...], right(dev))
                return carry

            lax.fori_loop(0, 4, block, 0)
            if half == 0:
                self.send0(t)


RING_SCRATCH = [
    pltpu.VMEM((PA_SLOTS, 2, 2, 2, TILE, TILE), F32),
    pltpu.VMEM((R0_SLOTS, 2, 2, TILE, TILE), F32),
    pltpu.VMEM((R1_SLOTS, 2, TILE, TILE), F32),
    pltpu.VMEM((R2_SLOTS, TILE, TILE), F32),
    pltpu.SemaphoreType.DMA((R0_SLOTS,)), pltpu.SemaphoreType.DMA((R0_SLOTS,)),
    pltpu.SemaphoreType.DMA((R1_SLOTS,)), pltpu.SemaphoreType.DMA((R1_SLOTS,)),
    pltpu.SemaphoreType.DMA((R2_SLOTS,)), pltpu.SemaphoreType.DMA((R2_SLOTS,)),
    pltpu.SemaphoreType.REGULAR, pltpu.SemaphoreType.REGULAR, pltpu.SemaphoreType.REGULAR,
]


LAG_F, LAG_H, LAG_I = 5, 6, 7


def corr_kernel(zh, zn_hbm, inv, lam, dz, loss_out,
                zn, acc, gt, lt, loss_acc, st, zn_sem, ssem, rsem,
                es, er, fs, fr, hs, hr, *ring_refs):
    me = lax.axis_index("data")
    zn_copy = pltpu.make_async_copy(zn_hbm, zn, zn_sem)
    zn_copy.start()
    entry_barrier(me)
    ring = Ring(me, TILES, *ring_refs[:4], ring_refs[4:10], ring_refs[10:])
    core, f, s = ring.core, ring.f, ring.s
    lam_val = lam[0, 0]
    acc[...] = jnp.zeros_like(acc)
    loss_acc[...] = jnp.zeros_like(loss_acc)

    def copy_e(t):
        block = gt.at[t, core, f, s]
        return ring.copy(block, block, es.at[t], er.at[t], ring.second)

    def copy_f(t):
        block = gt.at[t, core, f]
        return ring.copy(block, block, fs.at[t], fr.at[t], ring.first)

    def copy_h(t):
        block = gt.at[t, core]
        return ring.copy(block, block, hs.at[t], hr.at[t], ring.partner)

    def stage_a(t):
        lt[...] = zh[pl.ds(VIEW, VIEW), cols(t)].T
        ring.partial(t, lt, lambda dev: zh[pl.ds(0, VIEW), cols(dev)])
        ring.stage_b(t)

    def stage_d(t):
        corr = ring.stage_d(t) * (1.0 / TOTAL_ROWS)
        diag = (lax.broadcasted_iota(jnp.int32, corr.shape, 0) + TILE * t
                == lax.broadcasted_iota(jnp.int32, corr.shape, 1) + TILE * me)
        gap = 1.0 - corr
        loss_acc[...] += jnp.sum(jnp.where(diag, gap * gap, lam_val * corr * corr), axis=0, keepdims=True)
        grad = jnp.where(diag, -2.0 * gap, (2.0 * lam_val) * corr)
        gt[t, core, f, s] = (grad * (1.0 / TOTAL_ROWS)).astype(BF16)
        copy_e(t).start()

    def stage_f(t):
        copy_e(t).wait()
        copy_f(t).start()

    def stage_h(t):
        copy_f(t).wait()
        copy_h(t).start()

    def stage_i(t):
        copy_h(t).wait()

        def block(k, carry):
            c, a, b = k // 4, (k // 2) % 2, k % 2
            dev = c + a * (2 + 2 * c) + b * (4 - 2 * c)
            grad = gt[t, c, a, b]
            acc[dev, pl.ds(0, VIEW), :] += dot_nn(zh[pl.ds(VIEW, VIEW), cols(t)], grad)
            acc[t, pl.ds(VIEW, VIEW), :] += dot_nt(zh[pl.ds(0, VIEW), cols(dev)], grad)
            return carry

        lax.fori_loop(0, 8, block, 0)

    def tick(t, carry):
        for lag, stage in ((0, stage_a), (LAG_C, ring.stage_c), (LAG_D, stage_d), (LAG_F, stage_f),
                           (LAG_H, stage_h), (LAG_I, stage_i)):
            item = t - lag
            pl.when((item >= 0) & (item < TILES))(functools.partial(stage, item))
        return carry

    lax.fori_loop(0, TILES + LAG_I, tick, 0)
    st[TILES, 0] = jnp.zeros((4, TILE), F32)
    st[TILES, 0, pl.ds(0, 1), :] = loss_acc[...]
    stats_send(me, st, ssem, rsem, TILES)
    zn_copy.wait()

    def sums(q, carry):
        grad = acc[q]
        stats_put(st, q, grad, grad * zn[q])
        stats_send(me, st, ssem, rsem, q)
        return carry

    lax.fori_loop(0, TILES, sums, 0)

    def norm(q, carry):
        stats_wait(st, ssem, rsem, q)
        total = stats_total(st, q) * (1.0 / TOTAL_ROWS)
        for v in range(2):
            rows = pl.ds(v * VIEW, VIEW)
            grad = acc[q, rows, :] - (total[2 * v:2 * v + 1] + zn[q, rows, :] * total[2 * v + 1:2 * v + 2])
            dz[rows, cols(q)] = (inv[2, q, pl.ds(v, 1), :] * grad).astype(BF16)
        return carry

    lax.fori_loop(0, TILES, norm, 0)
    stats_wait(st, ssem, rsem, TILES)
    loss_out[...] = jnp.broadcast_to(jnp.sum(stats_total(st, TILES), keepdims=True), loss_out.shape)


ITEMS = 2 * TILES + 2
LAST_ROWS = 4 * PIECE


def backward_kernel(dz, x2, x1, h_a, h_b, w3_hbm, w2_hbm, xh2_hbm, xh1_hbm, inv, g1, b1, g2, b2,
                    dw_hbm, dw1, sums_out,
                    du2, du1, ht, lt, wt, xh, gpre, stage, st,
                    w_sem, xh_sem, out_sem, ssem, rsem, *ring_refs):
    me = lax.axis_index("data")
    entry_barrier(me)
    ring = Ring(me, ITEMS, *ring_refs[:4], ring_refs[4:10], ring_refs[10:])

    def out_copy(t):
        return pltpu.make_async_copy(stage.at[t % 2], dw_hbm.at[t // TILES, :, cols(t % TILES)], out_sem.at[t % 2])

    def store_out(t):
        when_in(t >= 2, lambda: out_copy(t - 2).wait())
        stage[t % 2] = ring.stage_d(t).T
        out_copy(t).start()

    for g in range(2):
        left, right, grad_out = ((dz, x2, du2), (du2, x1, du1))[g]
        w_hbm, xh_hbm = ((w3_hbm, xh2_hbm), (w2_hbm, xh1_hbm))[g]
        gain_ref, shift_ref = ((g2, b2), (g1, b1))[g]
        base = g * TILES

        def w_copy(e, w_hbm=w_hbm):
            rows = e * TILE if isinstance(e, int) else pl.multiple_of(e * TILE, TILE)
            return pltpu.make_async_copy(w_hbm.at[pl.ds(rows, TILE), :], wt.at[e % 2], w_sem.at[e % 2])

        def xh_copy(e, xh_hbm=xh_hbm):
            return pltpu.make_async_copy(xh_hbm.at[e], xh.at[e % 4], xh_sem.at[e % 4])

        def fetch(e, w_copy=w_copy, xh_copy=xh_copy):
            w_copy(e).start()
            xh_copy(e).start()

        fetch(0)
        fetch(1)

        def grad_tile(e, left=left, w_copy=w_copy, xh_copy=xh_copy, base=base,
                      gain_ref=gain_ref, shift_ref=shift_ref):
            w_copy(e).wait()
            xh_copy(e).wait()
            grad = dot_nt(left[...], wt[e % 2])
            normed = xh[e % 4]
            pre = gain_ref[:, cols(e)] * normed + shift_ref[:, cols(e)]
            grad = jnp.where(pre > 0, grad, 0.0)
            gpre[e % 3] = grad
            stats_put(st, base + e, grad, grad * normed)
            stats_send(me, st, ssem, rsem, base + e)

        def norm_tile(e, g=g, base=base, grad_out=grad_out, gain_ref=gain_ref):
            stats_wait(st, ssem, rsem, base + e)
            total = stats_total(st, base + e)
            for k in range(2):
                sums_out[pl.ds(2 * g + k, 1), cols(e)] = total[k:k + 1] + total[k + 2:k + 3]
            total = total * (1.0 / TOTAL_ROWS)
            for v in range(2):
                rows = pl.ds(v * VIEW, VIEW)
                grad = gpre[e % 3, rows, :] - (
                    total[2 * v:2 * v + 1] + xh[e % 4, rows, :] * total[2 * v + 1:2 * v + 2])
                scale = gain_ref[:, cols(e)] * inv[1 - g, e, pl.ds(v, 1), :]
                grad_out[rows, cols(e)] = (scale * grad).astype(BF16)

        def tick(q, carry, g=g, base=base, left=left, right=right,
                 grad_tile=grad_tile, norm_tile=norm_tile, fetch=fetch):
            t = base + q
            lt[...] = left[:, cols(q)].T
            ring.partial(t, lt, lambda dev: right[:, cols(dev)])

            def step(k, carry):
                e = 2 * q + k
                pl.when(e < TILES)(lambda: grad_tile(e))

                @pl.when(e >= 2)
                def _():
                    norm_tile(e - 2)

                pl.when(e + 2 < TILES)(lambda: fetch(e + 2))
                return carry

            @pl.when(q <= TILES // 2)
            def _():
                lax.fori_loop(0, 2, step, 0)

            ring.stage_b(t)
            pl.when(t >= LAG_C)(lambda: ring.stage_c(t - LAG_C))
            pl.when(t >= LAG_D)(lambda: store_out(t - LAG_D))
            return carry

        lax.fori_loop(0, TILES, tick, 0)

    ht[:, pl.ds(0, VIEW)] = h_a[...].T
    ht[:, pl.ds(VIEW, VIEW)] = h_b[...].T

    def rows_of(t):
        return LAST_ROWS if t >= 2 * TILES else TILE

    for t in range(2 * TILES, ITEMS + LAG_D):
        if t < ITEMS:
            for m in range(4):
                part = dot_nn(ht[...], du1[:, cols((t - 2 * TILES) * 4 + m)])
                for dev in range(8):
                    c, x, y = dev % 2, (dev // 2) % 2, dev // 4
                    a, b = (y, x) if c else (x, y)
                    ring.pa[t % PA_SLOTS, c, a, b, m * PIECE:(m + 1) * PIECE] = part[dev * PIECE:(dev + 1) * PIECE]
            ring.send0(t, LAST_ROWS)
            ring.stage_b(t, LAST_ROWS)
        if t - LAG_C < ITEMS:
            ring.stage_c(t - LAG_C, rows_of(t - LAG_C))
        d = t - LAG_D
        if d < 2 * TILES:
            store_out(d)
        else:
            total = ring.stage_d(d, LAST_ROWS)
            for m in range(4):
                dw1[:, cols((d - 2 * TILES) * 4 + m)] = total[m * PIECE:(m + 1) * PIECE]
    for t in (2 * TILES - 2, 2 * TILES - 1):
        out_copy(t).wait()


VMEM_SPEC = pl.BlockSpec(memory_space=pltpu.VMEM)
ANY_SPEC = pl.BlockSpec(memory_space=pl.ANY)
SMEM_SPEC = pl.BlockSpec(memory_space=pltpu.SMEM)
DMA = pltpu.SemaphoreType.DMA


def params(collective_id):
    return pltpu.CompilerParams(collective_id=collective_id, has_side_effects=True, vmem_limit_bytes=64_000_000)


def solution(mesh):
    sds = jax.ShapeDtypeStruct
    normed = sds((TILES, ROWS, TILE), F32)
    act = sds((ROWS, WIDTH), BF16)

    def local_step(h_a, h_b, w_one, w_two, w_three, gain_one, shift_one, gain_two, shift_two, lam_off):
        g1, b1, g2, b2 = (v.reshape(1, WIDTH) for v in (gain_one, shift_one, gain_two, shift_two))
        x1, x2, zh, inv, xh1, xh2, zn = pl.pallas_call(
            forward_kernel,
            out_shape=(act, act, act, sds((3, TILES, 2, TILE), F32), normed, normed, normed),
            in_specs=[VMEM_SPEC] * 2 + [ANY_SPEC] * 3 + [VMEM_SPEC] * 4,
            out_specs=(VMEM_SPEC,) * 4 + (ANY_SPEC,) * 3,
            scratch_shapes=[
                pltpu.VMEM((FEAT, WIDTH), BF16), pltpu.VMEM((2, TILES, WIDTH, TILE), BF16),
                pltpu.VMEM((TILES, ROWS, TILE), F32), pltpu.VMEM((3 * TILES, 8, 4, TILE), F32),
                DMA, DMA((2, TILES)), DMA((TILES,)), DMA((3 * TILES,)), DMA((3 * TILES,)),
            ],
            compiler_params=params(0), name="forward",
        )(h_a, h_b, w_one, w_two, w_three, g1, b1, g2, b2)
        dz, loss = pl.pallas_call(
            corr_kernel,
            out_shape=(act, sds((8, 128), F32)),
            in_specs=[VMEM_SPEC, ANY_SPEC, VMEM_SPEC, SMEM_SPEC],
            out_specs=(VMEM_SPEC, VMEM_SPEC),
            scratch_shapes=[
                pltpu.VMEM((TILES, ROWS, TILE), F32), pltpu.VMEM((TILES, ROWS, TILE), F32),
                pltpu.VMEM((TILES, 2, 2, 2, TILE, TILE), BF16), pltpu.VMEM((TILE, VIEW), BF16),
                pltpu.VMEM((1, TILE), F32), pltpu.VMEM((TILES + 1, 8, 4, TILE), F32),
                DMA, DMA((TILES + 1,)), DMA((TILES + 1,)),
            ] + [DMA((TILES,))] * 6 + RING_SCRATCH,
            compiler_params=params(1), name="corr",
        )(zh, zn, inv, lam_off.reshape(1, 1))
        dw, dw1, sums = pl.pallas_call(
            backward_kernel,
            out_shape=(sds((2, TILE, WIDTH), F32), sds((PIECE, WIDTH), F32), sds((4, WIDTH), F32)),
            in_specs=[VMEM_SPEC] * 5 + [ANY_SPEC] * 4 + [VMEM_SPEC] * 5,
            out_specs=(ANY_SPEC, VMEM_SPEC, VMEM_SPEC),
            scratch_shapes=[
                pltpu.VMEM((ROWS, WIDTH), BF16), pltpu.VMEM((ROWS, WIDTH), BF16),
                pltpu.VMEM((FEAT, ROWS), BF16), pltpu.VMEM((TILE, ROWS), BF16),
                pltpu.VMEM((2, TILE, WIDTH), BF16), pltpu.VMEM((4, ROWS, TILE), F32),
                pltpu.VMEM((3, ROWS, TILE), F32), pltpu.VMEM((2, TILE, TILE), F32),
                pltpu.VMEM((2 * TILES, 8, 4, TILE), F32),
                DMA((2,)), DMA((4,)), DMA((2,)), DMA((2 * TILES,)), DMA((2 * TILES,)),
            ] + RING_SCRATCH,
            compiler_params=params(2), name="backward",
        )(dz, x2, x1, h_a, h_b, w_three, w_two, xh2, xh1, inv, g1, b1, g2, b2)
        return (loss[0, 0], dw1, dw[1], dw[0], sums[3], sums[2], sums[1], sums[0])

    row_spec = P("data", None)
    whole_mat = P(None, None)
    whole_vec = P(None)
    return jax.shard_map(
        local_step, mesh=mesh,
        in_specs=(row_spec, row_spec, whole_mat, whole_mat, whole_mat,
                  whole_vec, whole_vec, whole_vec, whole_vec, P()),
        out_specs=(P(), row_spec, row_spec, row_spec, whole_vec, whole_vec, whole_vec, whole_vec),
        check_vma=False)
```

time: 788 us -> 361 us (0.46); the launches traced: 779 us -> 361 us
  waiting for transfers between devices: 427 us -> 0 us
  Pallas kernels: 0 us -> 352 us
  blocking collectives: 153 us -> 0 us
  matrix products: 137 us -> 0 us
  other arithmetic: 40.9 us -> 0 us
  between operations: 15.1 us -> 1.31 us
    pallas_call x0 -> x3, Pallas kernels: none -> 352 us  [the longest x1 171 us: local_step(): pl.pallas_call(backward_kernel, out_shape=(sds((2, TILE, WIDTH), F32), sd...]
    reduce_scatter x3 -> x0, waiting for transfers between devices: 220 us -> none  [the longest x1 111 us: local_step(): lax.psum_scatter(lax.dot_general(act_one, grad_hidden_two, ROW_DIMS, pref...]
    psum x1 -> x0, waiting for transfers between devices: 206 us -> none  [local_step(): corr_mat = lax.psum(corr_part, 'data') / total_rows]
    psum x6 -> x0, blocking collectives: 153 us -> none  [the longest x3 80.6 us: norm_backward(): lax.psum(jnp.stack([jnp.sum(grad_out, axis=1), jnp.sum(grad_out * normed,...]
    dot_general x11 -> x0, matrix products: 137 us -> none  [the longest x1 17.4 us: local_step(): lax.dot_general(grad_proj, w_three, LAST_DIMS, preferred_element_type=jnp...]
    convert_element_type x4 -> x0, other arithmetic: 25.9 us -> none  [the longest x1 7.15 us: local_step(): (gain_one * grad_hidden_one).astype(jnp.bfloat16).reshape(2 * rows_dev, -1)]
    reduce_sum x4 -> x0, other arithmetic: 14.7 us -> none  [the longest x1 8.86 us: local_step(): jnp.sum(jnp.where(diag_mask, diag_gap * diag_gap, lam_off * corr_mat * co...]
  transfers between devices with their start and end apart: 4 -> 0, of which waited for: 3 -> 0; matrix products, arithmetic and copies ran while one was open for 5% -> 0% of each run, Pallas kernels for 0% -> 0%
where the time goes in v1:
time: 361 us
  Pallas kernels  352 us (98%)
  local copies, waits for them, and re-layouts  8.25 us (2%)
    pallas_call x1, Pallas kernels, local_step(): pl.pallas_call(backward_kernel, out_shape=(sds((2, TILE, WIDTH), F32), sd...  171 us
    pallas_call x1, Pallas kernels, local_step(): pl.pallas_call(corr_kernel, out_shape=(act, sds((8, 128), F32)), in_specs...  130 us
    pallas_call x1, Pallas kernels, local_step(): pl.pallas_call(forward_kernel, out_shape=(act, act, act, sds((3, TILES, 2...  50.4 us

profile of v1, /device:TPU:0, one launch (start us, length us, event | category | flops | bytes accessed | tf_op | source)
XLA Modules:
  0.0 361.2 jit_solution(4312832715323683688)
XLA Ops:
  1.3 50.4 %forward.1 = (bf16[1024,2048]{1,0:T(8,128)(2,1)}, bf16[1024,2048]{1,0:T(8,128)(2,1)}, bf16[1024,2048]{1,0:T(8,128)(2,1)}, f32[3,8,2,256]{3,2,1,0:T(2,128)}, f32[...) custom-call(bf16[512,384]{1,0:T(8,128)(2,1)} %h_a.3, bf16[512,384]{1,0:T(8,128)(2,1)} %h_b.3, ...), custom_call_target="tpu_custom_call" | custom-call | tf_op jit(solution)/shard_map/forward/pallas_call | solution.py:488
  51.7 130.3 %corr.1 = (bf16[1024,2048]{1,0:T(8,128)(2,1)}, f32[8,128]{1,0:T(8,128)}) custom-call(bf16[1024,2048]{1,0:T(8,128)(2,1)} %get-tuple-element.20.zh, f32[8,1024,256]{2,1,0:T(8,128)} %get-tuple-element.21.zn_hbm, f32[3,8,2,256]{3,2,1,0:T(2,128)} %get-tuple-element.22.inv, f32[1,1]{1,0:T(1,128)} %bitcast.14.lam), custom_call_target="tpu_custom_call" | custom-call | tf_op jit(solution)/shard_map/corr/pallas_call | solution.py:500
  182.0 171.0 %backward.1 = (f32[2,256,2048]{2,1,0:T(8,128)}, f32[48,2048]{1,0:T(8,128)}, f32[4,2048]{1,0:T(4,128)}) custom-call(bf16[1024,2048]{1,0:T(8,128)(2,1)} %get-tuple-element.24.dz, bf16[1024,2048]{1,0:T(8,128)(2,1)} %get-tuple-element.25.x2, bf16[1024,2048]{1,0:T(8,128)(2,1)} %get-tuple-element.26.x1, bf16[512,384]{1,0:T(8,128)(2,1)} %h_a.3, ...), custom_call_target="tpu_custom_call" | custom-call | tf_op jit(solution)/shard_map/backward/pallas_call | solution.py:513
  353.0 1.2 slice.21
  354.2 1.5 fusion
  355.7 0.0 copy-start
  355.7 4.8 %slice_bitcast_fusion = (f32[256,2048]{1,0:T(8,128)}, f32[256,2048]{1,0:T(8,128)}) fusion(f32[2,256,2048]{2,1,0:T(8,128)} %get-tuple-element.30), kind=kLoop, calls=%fused_computation | loop fusion | bytes 8388608 | tf_op jit(solution)/shard_map/squeeze | solution.py:528
  360.5 0.0 copy-done
  360.5 0.7 copy.20
Async XLA Ops:
  355.7 4.8 %copy-start = (f32[48,2048]{1,0:T(8,128)S(1)}, f32[48,2048]{1,0:T(8,128)}, u32[]{:S(2)}) copy-start(f32[48,2048]{1,0:T(8,128)} %get-tuple-element.47) | copy-start | bytes 1179652

commit v2 on v1

v2 whole, which is shorter than its diff:
```python
import functools

import jax
import jax.numpy as jnp
from jax import lax
from jax.experimental import pallas as pl
from jax.experimental.pallas import tpu as pltpu
from jax.sharding import PartitionSpec as P

MESH = pl.DeviceIdType.MESH
F32, BF16 = jnp.float32, jnp.bfloat16
NORM_EPS = 1e-5
TOTAL_ROWS = 4096
VIEW = 512
ROWS = 2 * VIEW
FEAT = 384
WIDTH = 2048
TILE = 256
TILES = WIDTH // TILE
FWD_TILE = 512
FWD_TILES = WIDTH // FWD_TILE
PIECE = FEAT // 8
CHUNK = 128
CHUNKS = WIDTH // CHUNK
PAIRS = CHUNKS // 2
LAG_C, LAG_D, LAG_F, LAG_H, LAG_I = 1, 2, 3, 4, 5
PA_SLOTS, R0_SLOTS, R1_SLOTS, R2_SLOTS = 6, 2, 4, 4


def dot_nn(a, b):
    return jnp.dot(a, b, preferred_element_type=F32)


def dot_nt(a, b):
    return lax.dot_general(a, b, (((1,), (1,)), ((), ())), preferred_element_type=F32)


def when_in(cond, fn):
    if isinstance(cond, bool):
        if cond:
            fn()
    else:
        pl.when(cond)(fn)


def peer_of(me, r):
    out = me
    for bit in (1, 2, 4):
        if r & bit:
            out = out + bit - 2 * bit * ((me // bit) % 2)
    return out


def barrier_signal(me):
    for r in range(1, 8):
        pl.semaphore_signal(pltpu.get_barrier_semaphore(), inc=1, device_id=(peer_of(me, r),), device_id_type=MESH)


def barrier_wait():
    pl.semaphore_wait(pltpu.get_barrier_semaphore(), 7)


def cols(t, width=TILE):
    if isinstance(t, int):
        return pl.ds(t * width, width)
    return pl.ds(pl.multiple_of(t * width, width), width)


def fcols(t):
    return cols(t, FWD_TILE)


def stats_send(me, st, ssem, rsem, i):
    for r in range(1, 8):
        pltpu.make_async_remote_copy(
            src_ref=st.at[i, 0], dst_ref=st.at[i, r], send_sem=ssem.at[i], recv_sem=rsem.at[i],
            device_id=(peer_of(me, r),), device_id_type=MESH).start()


def stats_wait(st, ssem, rsem, i):
    block = st.at[i, pl.ds(1, 7)]
    pltpu.make_async_copy(block, block, rsem.at[i]).wait()
    pltpu.make_async_copy(block, block, ssem.at[i]).wait()


def stats_total(st, i):
    pairs = [st[i, 2 * k] + st[i, 2 * k + 1] for k in range(4)]
    return (pairs[0] + pairs[1]) + (pairs[2] + pairs[3])


def stats_put(st, i, values, weighted):
    for v in range(values.shape[0] // VIEW):
        part = slice(v * VIEW, (v + 1) * VIEW)
        st[i, 0, pl.ds(2 * v, 1), :] = jnp.sum(values[part], axis=0, keepdims=True)
        st[i, 0, pl.ds(2 * v + 1, 1), :] = jnp.sum(weighted[part], axis=0, keepdims=True)


def forward_kernel(h_a, h_b, w1_hbm, w2_hbm, w3_hbm, g1, b1, g2, b2,
                   inv_out, x1_hbm, x2_hbm, zh_hbm, xh1_hbm, xh2_hbm, zn_hbm,
                   x1, x2, zh, w1, wb, u, st, w1_sem, w_sem, norm_sem, act_sem, ssem, rsem):
    me = lax.axis_index("data")
    w1_copy = pltpu.make_async_copy(w1_hbm, w1, w1_sem)
    w1_copy.start()

    def w_copy(layer):
        return pltpu.make_async_copy((w2_hbm, w3_hbm)[layer], wb.at[layer], w_sem.at[layer])

    for layer in range(2):
        w_copy(layer).start()
    barrier_signal(me)
    barrier_wait()
    w1_copy.wait()

    acts = (x1, x2, zh)
    acts_hbm = (x1_hbm, x2_hbm, zh_hbm)
    normed_hbm = (xh1_hbm, xh2_hbm, zn_hbm)

    def rows_of(v):
        return pl.ds(v * VIEW, VIEW)

    def norm_copy(layer, v, q):
        return pltpu.make_async_copy(u.at[v, q], normed_hbm[layer].at[v, q], norm_sem.at[v, q])

    def act_copy(layer, v):
        return pltpu.make_async_copy(acts[layer].at[rows_of(v)], acts_hbm[layer].at[rows_of(v)], act_sem.at[layer, v])

    def slot(layer, v, q):
        return (2 * layer + v) * FWD_TILES + q

    def run(matmul=None, norm=None):
        def body(q, carry):
            if matmul is not None:
                layer, v = matmul
                if layer > 0:
                    norm_copy(layer - 1, v, q).wait()
            if norm is not None:
                n_layer, n_view = norm
                stats_wait(st, ssem, rsem, slot(n_layer, n_view, q))
            if matmul is not None:
                if layer > 0:
                    vals = dot_nn(acts[layer - 1][rows_of(v), :], wb[layer - 1, :, fcols(q)])
                else:
                    vals = dot_nn((h_a, h_b)[v][...], w1[:, fcols(q)])
            if norm is not None:
                total = stats_total(st, slot(n_layer, n_view, q)) * (1.0 / TOTAL_ROWS)
                mean = total[0:1]
                inv = lax.rsqrt(total[1:2] - mean * mean + NORM_EPS)
                inv_out[n_layer, n_view, q] = inv
                normed = (u[n_view, q] - mean) * inv
                u[n_view, q] = normed
                if n_layer < 2:
                    gain, shift = ((g1, b1), (g2, b2))[n_layer]
                    normed = jnp.maximum(gain[:, fcols(q)] * normed + shift[:, fcols(q)], 0.0)
                acts[n_layer][rows_of(n_view), fcols(q)] = normed.astype(BF16)
            if matmul is not None:
                u[v, q] = vals
                st[slot(layer, v, q), 0, pl.ds(0, 1), :] = jnp.sum(vals, axis=0, keepdims=True)
                st[slot(layer, v, q), 0, pl.ds(1, 1), :] = jnp.sum(vals * vals, axis=0, keepdims=True)
                stats_send(me, st, ssem, rsem, slot(layer, v, q))
            if norm is not None:
                norm_copy(n_layer, n_view, q).start()
            return carry

        if matmul in ((1, 0), (2, 0)):
            w_copy(matmul[0] - 1).wait()
        lax.fori_loop(0, FWD_TILES, body, 0)
        if norm is not None:
            act_copy(*norm).start()

    run(matmul=(0, 0))
    run(matmul=(0, 1))
    run(norm=(0, 0))
    run(matmul=(1, 0), norm=(0, 1))
    run(matmul=(1, 1), norm=(1, 0))
    run(matmul=(2, 0), norm=(1, 1))
    run(matmul=(2, 1), norm=(2, 0))
    run(norm=(2, 1))
    for v in range(2):
        for q in range(FWD_TILES):
            norm_copy(2, v, q).wait()
        for layer in range(3):
            act_copy(layer, v).wait()


class Ring:
    def __init__(self, me, items, pa, r0, r1, r2, sems, credits):
        self.items, self.pa, self.r0, self.r1, self.r2 = items, pa, r0, r1, r2
        self.s0, self.q0, self.s1, self.q1, self.s2, self.q2 = sems
        self.c0, self.c1, self.c2 = credits
        core = me % 2
        x, y = (me // 2) % 2, me // 4
        self.core = core
        self.f = x + core * (y - x)
        self.s = y + core * (x - y)
        x_side, y_side = me + 2 - 4 * x, me + 4 - 8 * y
        self.partner = me + 1 - 2 * core
        self.first = x_side + core * (y_side - x_side)
        self.second = y_side + core * (x_side - y_side)

    def copy(self, src, dst, send, recv, device):
        return pltpu.make_async_remote_copy(src_ref=src, dst_ref=dst, send_sem=send, recv_sem=recv,
                                            device_id=(device,), device_id_type=MESH)

    def copy0(self, t, rows):
        return self.copy(self.pa.at[t % PA_SLOTS, 1 - self.core, :, :, pl.ds(0, rows)],
                         self.r0.at[t % R0_SLOTS, :, :, pl.ds(0, rows)],
                         self.s0.at[t % R0_SLOTS], self.q0.at[t % R0_SLOTS], self.partner)

    def copy1(self, t, rows):
        return self.copy(self.pa.at[t % PA_SLOTS, self.core, 1 - self.f, :, pl.ds(0, rows)],
                         self.r1.at[t % R1_SLOTS, :, pl.ds(0, rows)],
                         self.s1.at[t % R1_SLOTS], self.q1.at[t % R1_SLOTS], self.first)

    def copy2(self, t, rows):
        return self.copy(self.pa.at[t % PA_SLOTS, self.core, self.f, 1 - self.s, pl.ds(0, rows)],
                         self.r2.at[t % R2_SLOTS, pl.ds(0, rows)],
                         self.s2.at[t % R2_SLOTS], self.q2.at[t % R2_SLOTS], self.second)

    def take_credit(self, sem, t, slots):
        when_in(t >= slots, lambda: pl.semaphore_wait(sem, 1))

    def give_credit(self, sem, t, slots, device):
        when_in(t + slots < self.items,
                lambda: pl.semaphore_signal(sem, inc=1, device_id=(device,), device_id_type=MESH))

    def send0(self, t, rows=CHUNK):
        self.take_credit(self.c0, t, R0_SLOTS)
        self.copy0(t, rows).start()

    def stage_b(self, t, rows=CHUNK):
        self.copy0(t, rows).wait()
        slot = t % PA_SLOTS
        for k in range(4):
            a, b = k // 2, k % 2
            self.pa[slot, self.core, a, b, :rows] += self.r0[t % R0_SLOTS, a, b, :rows]
        self.give_credit(self.c0, t, R0_SLOTS, self.partner)
        self.take_credit(self.c1, t, R1_SLOTS)
        self.copy1(t, rows).start()

    def stage_c(self, t, rows=CHUNK):
        self.copy1(t, rows).wait()
        slot = t % PA_SLOTS
        for b in range(2):
            self.pa[slot, self.core, self.f, b, :rows] += self.r1[t % R1_SLOTS, b, :rows]
        self.give_credit(self.c1, t, R1_SLOTS, self.first)
        self.take_credit(self.c2, t, R2_SLOTS)
        self.copy2(t, rows).start()

    def stage_d(self, t, rows=CHUNK):
        self.copy2(t, rows).wait()
        total = self.pa[t % PA_SLOTS, self.core, self.f, self.s, :rows] + self.r2[t % R2_SLOTS, :rows]
        self.give_credit(self.c2, t, R2_SLOTS, self.second)
        return total

    def partial(self, p, lt, right):
        for chip in range(4):
            part = dot_nn(lt, right[:, pl.ds(2 * chip * TILE, 2 * TILE)])
            x, y = chip % 2, chip // 2
            for c in range(2):
                a, b = (y, x) if c else (x, y)
                for k in range(2):
                    self.pa[(2 * p + k) % PA_SLOTS, c, a, b] = part[k * CHUNK:(k + 1) * CHUNK, c * TILE:(c + 1) * TILE]
        self.send0(2 * p)
        self.send0(2 * p + 1)


RING_SCRATCH = [
    pltpu.VMEM((PA_SLOTS, 2, 2, 2, CHUNK, TILE), F32),
    pltpu.VMEM((R0_SLOTS, 2, 2, CHUNK, TILE), F32),
    pltpu.VMEM((R1_SLOTS, 2, CHUNK, TILE), F32),
    pltpu.VMEM((R2_SLOTS, CHUNK, TILE), F32),
    pltpu.SemaphoreType.DMA((R0_SLOTS,)), pltpu.SemaphoreType.DMA((R0_SLOTS,)),
    pltpu.SemaphoreType.DMA((R1_SLOTS,)), pltpu.SemaphoreType.DMA((R1_SLOTS,)),
    pltpu.SemaphoreType.DMA((R2_SLOTS,)), pltpu.SemaphoreType.DMA((R2_SLOTS,)),
    pltpu.SemaphoreType.REGULAR, pltpu.SemaphoreType.REGULAR, pltpu.SemaphoreType.REGULAR,
]


LAST_COLS = 512
LAST_ITEMS = WIDTH // LAST_COLS
LAST_ROWS = LAST_COLS // TILE * PIECE
FIRST_LAST = 3 * CHUNKS
ITEMS = FIRST_LAST + LAST_ITEMS
NORM_LAG = 4
ST_LOSS = 4 * TILES


def main_kernel(zh_hbm, zn_hbm, x2_hbm, x1_hbm, h_a, h_b, w3_hbm, w2_hbm, xh2_hbm, xh1_hbm,
                inv, g1, b1, g2, b2, lam, dw3_hbm, dw2_hbm, small,
                z, normed, acc, gt, gbuf, x2, x1, du2, ht, lt, wt, stage, loss_acc, st,
                z_sem, normed_sem, x_sem, w_sem, out_sem, ssem, rsem,
                es, er, fs, fr, hs, hr, *ring_refs):
    me = lax.axis_index("data")
    z_copy = pltpu.make_async_copy(zh_hbm, z, z_sem)
    x2_copy = pltpu.make_async_copy(x2_hbm, x2, x_sem.at[0])
    x1_copy = pltpu.make_async_copy(x1_hbm, x1, x_sem.at[1])

    def normed_copies(src, sem):
        return [pltpu.make_async_copy(
            src.at[v, q // 2, :, cols(q % 2)], normed.at[q, pl.ds(v * VIEW, VIEW)], sem.at[v, q])
            for v in range(2) for q in range(TILES)]

    z_copy.start()
    barrier_signal(me)
    ring = Ring(me, ITEMS, *ring_refs[:4], ring_refs[4:10], ring_refs[10:])
    core, f, s = ring.core, ring.f, ring.s
    lam_val = lam[0, 0]
    acc[...] = jnp.zeros_like(acc)
    loss_acc[...] = jnp.zeros_like(loss_acc)
    barrier_wait()
    z_copy.wait()
    for copy in normed_copies(zn_hbm, normed_sem):
        copy.start()
    x2_copy.start()
    x1_copy.start()
    view_a, view_b = pl.ds(0, VIEW), pl.ds(VIEW, VIEW)

    def copy_e(t):
        block = gt.at[t, core, f, s]
        return ring.copy(block, block, es.at[t], er.at[t], ring.second)

    def copy_f(t):
        block = gt.at[t, core, f]
        return ring.copy(block, block, fs.at[t], fr.at[t], ring.first)

    def copy_h(t):
        block = gt.at[t, core]
        return ring.copy(block, block, hs.at[t], hr.at[t], ring.partner)

    def both(work):
        def run(p):
            work(2 * p)
            work(2 * p + 1)
        return run

    def corr_a(p):
        lt[:, view_a] = z[view_b, cols(p)].T
        ring.partial(p, lt[:, view_a], z.at[view_a])
        both(ring.stage_b)(p)

    def corr_d(t):
        corr = ring.stage_d(t) * (1.0 / TOTAL_ROWS)
        diag = (lax.broadcasted_iota(jnp.int32, corr.shape, 0) + CHUNK * t
                == lax.broadcasted_iota(jnp.int32, corr.shape, 1) + TILE * me)
        gap = 1.0 - corr
        loss_acc[...] += jnp.sum(jnp.where(diag, gap * gap, lam_val * corr * corr), axis=0, keepdims=True)
        grad = jnp.where(diag, -2.0 * gap, (2.0 * lam_val) * corr)
        gt[t, core, f, s] = (grad * (1.0 / TOTAL_ROWS)).astype(BF16)
        copy_e(t).start()

    def corr_f(t):
        copy_e(t).wait()
        copy_f(t).start()

    def corr_h(t):
        copy_f(t).wait()
        copy_h(t).start()

    def corr_i(p):
        both(lambda t: copy_h(t).wait())(p)
        for dev in range(8):
            c, x, y = dev % 2, (dev // 2) % 2, dev // 4
            a, b = (y, x) if c else (x, y)
            for k in range(2):
                gbuf[pl.ds(k * CHUNK, CHUNK), cols(dev)] = gt[2 * p + k, c, a, b]
        grad_b = dot_nt(z[view_a, :], gbuf[...])
        acc[p, view_b, :] = grad_b
        for k in range(4):
            part = dot_nn(z[view_b, cols(p)], gbuf[:, pl.ds(2 * k * TILE, 2 * TILE)])
            acc[2 * k, view_a, :] += part[:, :TILE]
            acc[2 * k + 1, view_a, :] += part[:, TILE:]
        both_views = normed_copies(zn_hbm, normed_sem)

        @pl.when(p == 0)
        def _():
            for copy in both_views:
                copy.wait()

        stats_put(st, TILES + p, grad_b, grad_b * normed[p, view_b, :])
        stats_send(me, st, ssem, rsem, TILES + p)

    def corr_tick(p, carry):
        for lag, work in ((0, corr_a), (LAG_C, both(ring.stage_c)), (LAG_D, both(corr_d)), (LAG_F, both(corr_f)),
                          (LAG_H, both(corr_h)), (LAG_I, corr_i)):
            item = p - lag
            pl.when((item >= 0) & (item < PAIRS))(functools.partial(work, item))
        return carry

    st[:, 0] = jnp.zeros((st.shape[0],) + st.shape[2:], F32)
    lax.fori_loop(0, PAIRS + LAG_I, corr_tick, 0)

    def out_sums(q, carry):
        grad = acc[q, view_a, :]
        stats_put(st, q, grad, grad * normed[q, view_a, :])
        stats_send(me, st, ssem, rsem, q)
        return carry

    lax.fori_loop(0, TILES, out_sums, 0)

    def out_norm(q, carry):
        for v in range(2):
            stats_wait(st, ssem, rsem, v * TILES + q)
            total = stats_total(st, v * TILES + q) * (1.0 / TOTAL_ROWS)
            rows = pl.ds(v * VIEW, VIEW)
            grad = acc[q, rows, :] - (total[0:1] + normed[q, rows, :] * total[1:2])
            z[rows, cols(q)] = (inv[2, v, q // 2, :, cols(q % 2)] * grad).astype(BF16)
        return carry

    out_norm(0, 0)
    x2_copy.wait()

    def out_copy(t, hbm):
        return pltpu.make_async_copy(stage.at[t % 2], hbm.at[:, cols(t % CHUNKS, CHUNK)], out_sem.at[t % 2])

    def store_out(t):
        when_in(t >= CHUNKS + 2, lambda: out_copy(t - 2, dw3_hbm).wait())
        stage[t % 2] = ring.stage_d(t).T
        if isinstance(t, int):
            out_copy(t, dw2_hbm if t >= 2 * CHUNKS else dw3_hbm).start()
        else:
            pl.when(t < 2 * CHUNKS)(lambda: out_copy(t, dw3_hbm).start())
            pl.when(t >= 2 * CHUNKS)(lambda: out_copy(t, dw2_hbm).start())

    gpre = acc
    for g in range(2):
        left, right, grad_out = ((z, x2, du2), (du2, x1, z))[g]
        w_hbm, xh_hbm = ((w3_hbm, xh2_hbm), (w2_hbm, xh1_hbm))[g]
        gain_ref, shift_ref = ((g2, b2), (g1, b1))[g]
        base = (2 + g) * TILES

        def w_copy(e, w_hbm=w_hbm):
            rows = e * TILE if isinstance(e, int) else pl.multiple_of(e * TILE, TILE)
            return pltpu.make_async_copy(w_hbm.at[pl.ds(rows, TILE), :], wt.at[e % 2], w_sem.at[e % 2])

        def grad_tile(e, left=left, w_copy=w_copy, base=base, gain_ref=gain_ref, shift_ref=shift_ref):
            w_copy(e).wait()
            grad = dot_nt(left[...], wt[e % 2])
            values = normed[e]
            pre = gain_ref[:, cols(e)] * values + shift_ref[:, cols(e)]
            grad = jnp.where(pre > 0, grad, 0.0)
            gpre[e] = grad
            stats_put(st, base + e, grad, grad * values)
            stats_send(me, st, ssem, rsem, base + e)

        def norm_tile(e, g=g, base=base, grad_out=grad_out, gain_ref=gain_ref):
            stats_wait(st, ssem, rsem, base + e)
            total = stats_total(st, base + e)
            for k in range(2):
                small[pl.ds(PIECE + 2 * g + k, 1), cols(e)] = total[k:k + 1] + total[k + 2:k + 3]
            total = total * (1.0 / TOTAL_ROWS)
            for v in range(2):
                rows = pl.ds(v * VIEW, VIEW)
                grad = gpre[e, rows, :] - (
                    total[2 * v:2 * v + 1] + normed[e, rows, :] * total[2 * v + 1:2 * v + 2])
                scale = gain_ref[:, cols(e)] * inv[1 - g, v, e // 2, :, cols(e % 2)]
                grad_out[rows, cols(e)] = (scale * grad).astype(BF16)

        def tick(q, carry, g=g, left=left, right=right, grad_tile=grad_tile, norm_tile=norm_tile, w_copy=w_copy,
                 xh_hbm=xh_hbm):
            p = (1 + g) * PAIRS + q
            lt[...] = left[:, cols(q)].T
            ring.partial(p, lt[...], right)

            @pl.when(q == 0)
            def _():
                if g == 0:
                    both(ring.stage_b)(p)
                    lax.fori_loop(1, TILES, out_norm, 0)
                w_copy(0).start()
                w_copy(1).start()
                for copy in normed_copies(xh_hbm, normed_sem):
                    copy.start()

            @pl.when(q == 1)
            def _():
                for copy in normed_copies(xh_hbm, normed_sem):
                    copy.wait()

            def step(k, carry):
                e = 2 * (q - 1) + k
                pl.when(e < TILES)(lambda: grad_tile(e))
                pl.when((e >= NORM_LAG) & (e < TILES + NORM_LAG))(lambda: norm_tile(e - NORM_LAG))
                pl.when(e + 2 < TILES)(lambda: w_copy(e + 2).start())
                return carry

            @pl.when(q >= 1)
            def _():
                lax.fori_loop(0, 2, step, 0)

            if g == 0:
                pl.when(q > 0)(lambda: both(ring.stage_b)(p))
                pl.when(q >= LAG_C)(lambda: both(ring.stage_c)(p - LAG_C))
                pl.when(q >= LAG_D)(lambda: both(store_out)(p - LAG_D))
            else:
                both(ring.stage_b)(p)
                both(ring.stage_c)(p - LAG_C)
                both(store_out)(p - LAG_D)
            return carry

        if g == 1:
            x1_copy.wait()
        lax.fori_loop(0, PAIRS, tick, 0)

    ht[:, view_a] = h_a[...].T
    ht[:, view_b] = h_b[...].T
    per_item = LAST_COLS // TILE

    def rows_of(t):
        return LAST_ROWS if t >= FIRST_LAST else CHUNK

    for t in range(FIRST_LAST, ITEMS + 2 * LAG_D):
        if t < ITEMS:
            for m in range(per_item):
                part = dot_nn(ht[...], z[:, cols((t - FIRST_LAST) * per_item + m)])
                for dev in range(8):
                    c, x, y = dev % 2, (dev // 2) % 2, dev // 4
                    a, b = (y, x) if c else (x, y)
                    ring.pa[t % PA_SLOTS, c, a, b, m * PIECE:(m + 1) * PIECE] = part[dev * PIECE:(dev + 1) * PIECE]
            ring.send0(t, LAST_ROWS)
            ring.stage_b(t, LAST_ROWS)
        if t - 2 * LAG_C < ITEMS:
            ring.stage_c(t - 2 * LAG_C, rows_of(t - 2 * LAG_C))
        d = t - 2 * LAG_D
        if d < FIRST_LAST:
            store_out(d)
        else:
            total = ring.stage_d(d, LAST_ROWS)
            for m in range(per_item):
                small[pl.ds(0, PIECE), cols((d - FIRST_LAST) * per_item + m)] = total[m * PIECE:(m + 1) * PIECE]
        if t == FIRST_LAST:
            st[ST_LOSS, 0, pl.ds(0, 1), :] = loss_acc[...]
            stats_send(me, st, ssem, rsem, ST_LOSS)
    for t in (FIRST_LAST - 2, FIRST_LAST - 1):
        out_copy(t, dw2_hbm).wait()
    stats_wait(st, ssem, rsem, ST_LOSS)
    loss = jnp.sum(stats_total(st, ST_LOSS), keepdims=True)
    small[pl.ds(PIECE + 4, 4), :] = jnp.broadcast_to(loss, (4, WIDTH))


def finish_kernel(dw3_in, dw2_in, small_in, dw1, dw2, dw3, gg1, gs1, gg2, gs2, loss, v3, v2, vs, in_sem, out_sem):
    loads = [pltpu.make_async_copy(small_in, vs, in_sem.at[0])]
    stores = [pltpu.make_async_copy(vs.at[pl.ds(0, PIECE)], dw1, out_sem.at[0])]
    for k, (src, mid, dst) in enumerate(((dw3_in, v3, dw3), (dw2_in, v2, dw2))):
        for part in range(4):
            rows = pl.ds(part * TILE // 4, TILE // 4)
            i = 1 + 4 * k + part
            loads.append(pltpu.make_async_copy(src.at[rows], mid.at[rows], in_sem.at[i]))
            stores.append(pltpu.make_async_copy(mid.at[rows], dst.at[rows], out_sem.at[i]))
    for load in loads:
        load.start()
    for load, store in zip(loads, stores):
        load.wait()
        store.start()
    for k, ref in enumerate((gs2, gg2, gs1, gg1)):
        ref[...] = vs[pl.ds(PIECE + k, 1), :]
    loss[...] = vs[pl.ds(PIECE + 4, 1), pl.ds(0, 1)]
    for store in stores:
        store.wait()


VMEM_SPEC = pl.BlockSpec(memory_space=pltpu.VMEM)
ANY_SPEC = pl.BlockSpec(memory_space=pl.ANY)
SMEM_SPEC = pl.BlockSpec(memory_space=pltpu.SMEM)
DMA = pltpu.SemaphoreType.DMA


def params(collective_id):
    return pltpu.CompilerParams(collective_id=collective_id, has_side_effects=True, vmem_limit_bytes=64_000_000)


def solution(mesh):
    sds = jax.ShapeDtypeStruct
    normed = sds((2, FWD_TILES, VIEW, FWD_TILE), F32)
    act = sds((ROWS, WIDTH), BF16)
    weight = sds((TILE, WIDTH), F32)
    vector = sds((1, WIDTH), F32)
    small = 2 * PIECE - 40

    def local_step(h_a, h_b, w_one, w_two, w_three, gain_one, shift_one, gain_two, shift_two, lam_off):
        g1, b1, g2, b2 = (v.reshape(1, WIDTH) for v in (gain_one, shift_one, gain_two, shift_two))
        inv, x1, x2, zh, xh1, xh2, zn = pl.pallas_call(
            forward_kernel,
            out_shape=(sds((3, 2, FWD_TILES, 1, FWD_TILE), F32), act, act, act, normed, normed, normed),
            in_specs=[VMEM_SPEC] * 2 + [ANY_SPEC] * 3 + [VMEM_SPEC] * 4,
            out_specs=(VMEM_SPEC,) + (ANY_SPEC,) * 6,
            scratch_shapes=[
                pltpu.VMEM((ROWS, WIDTH), BF16), pltpu.VMEM((ROWS, WIDTH), BF16), pltpu.VMEM((ROWS, WIDTH), BF16),
                pltpu.VMEM((FEAT, WIDTH), BF16), pltpu.VMEM((2, WIDTH, WIDTH), BF16),
                pltpu.VMEM((2, FWD_TILES, VIEW, FWD_TILE), F32), pltpu.VMEM((6 * FWD_TILES, 8, 2, FWD_TILE), F32),
                DMA, DMA((2,)), DMA((2, FWD_TILES)), DMA((3, 2)), DMA((6 * FWD_TILES,)), DMA((6 * FWD_TILES,)),
            ],
            compiler_params=params(0), name="forward",
        )(h_a, h_b, w_one, w_two, w_three, g1, b1, g2, b2)
        dw3, dw2, rest = pl.pallas_call(
            main_kernel,
            out_shape=(weight, weight, sds((small, WIDTH), F32)),
            in_specs=[ANY_SPEC] * 4 + [VMEM_SPEC] * 2 + [ANY_SPEC] * 4 + [VMEM_SPEC] * 5 + [SMEM_SPEC],
            out_specs=(ANY_SPEC, ANY_SPEC, VMEM_SPEC),
            scratch_shapes=[
                pltpu.VMEM((ROWS, WIDTH), BF16), pltpu.VMEM((TILES, ROWS, TILE), F32),
                pltpu.VMEM((TILES, ROWS, TILE), F32), pltpu.VMEM((CHUNKS, 2, 2, 2, CHUNK, TILE), BF16),
                pltpu.VMEM((TILE, WIDTH), BF16),
                pltpu.VMEM((ROWS, WIDTH), BF16), pltpu.VMEM((ROWS, WIDTH), BF16), pltpu.VMEM((ROWS, WIDTH), BF16),
                pltpu.VMEM((FEAT, ROWS), BF16), pltpu.VMEM((TILE, ROWS), BF16),
                pltpu.VMEM((2, TILE, WIDTH), BF16), pltpu.VMEM((2, TILE, CHUNK), F32),
                pltpu.VMEM((1, TILE), F32), pltpu.VMEM((ST_LOSS + 1, 8, 4, TILE), F32),
                DMA, DMA((2, TILES)), DMA((2,)), DMA((2,)), DMA((2,)), DMA((ST_LOSS + 1,)), DMA((ST_LOSS + 1,)),
            ] + [DMA((CHUNKS,))] * 6 + RING_SCRATCH,
            compiler_params=params(1), name="main",
        )(zh, zn, x2, x1, h_a, h_b, w_three, w_two, xh2, xh1, inv, g1, b1, g2, b2, lam_off.reshape(1, 1))
        dw1, dw2, dw3, gg1, gs1, gg2, gs2, loss = pl.pallas_call(
            finish_kernel,
            out_shape=(sds((PIECE, WIDTH), F32), weight, weight, vector, vector, vector, vector, sds((1, 1), F32)),
            in_specs=[ANY_SPEC] * 3,
            out_specs=(ANY_SPEC,) * 3 + (VMEM_SPEC,) * 5,
            scratch_shapes=[
                pltpu.VMEM((TILE, WIDTH), F32), pltpu.VMEM((TILE, WIDTH), F32), pltpu.VMEM((small, WIDTH), F32),
                DMA((9,)), DMA((9,)),
            ],
            compiler_params=pltpu.CompilerParams(vmem_limit_bytes=66_000_000), name="finish",
        )(dw3, dw2, rest)
        return (loss.reshape(()), dw1, dw2, dw3, gg1.reshape(WIDTH), gs1.reshape(WIDTH),
                gg2.reshape(WIDTH), gs2.reshape(WIDTH))

    row_spec = P("data", None)
    whole_mat = P(None, None)
    whole_vec = P(None)
    return jax.shard_map(
        local_step, mesh=mesh,
        in_specs=(row_spec, row_spec, whole_mat, whole_mat, whole_mat,
                  whole_vec, whole_vec, whole_vec, whole_vec, P()),
        out_specs=(P(), row_spec, row_spec, row_spec, whole_vec, whole_vec, whole_vec, whole_vec),
        check_vma=False)
```

time: 361 us -> 337 us (0.934)
  Pallas kernels: 352 us -> 336 us
  local copies, waits for them, and re-layouts: 8.25 us -> 0 us
    pallas_call x3, Pallas kernels: 352 us -> 336 us  [the longest x1 287 us: local_step(): pl.pallas_call(main_kernel, out_shape=(weight, weight, sds((small, WIDTH)...]
    squeeze x1 -> x0, local copies, waits for them, and re-layouts: 4.78 us -> none  [local_step(): return (loss[0, 0], dw1, dw[1], dw[0], sums[3], sums[2], sums[1], sums[0])]
where the time goes in v2:
time: 337 us
  Pallas kernels  336 us (100%)
    pallas_call x1, Pallas kernels, local_step(): pl.pallas_call(main_kernel, out_shape=(weight, weight, sds((small, WIDTH)...  287 us
    pallas_call x1, Pallas kernels, local_step(): pl.pallas_call(forward_kernel, out_shape=(sds((3, 2, FWD_TILES, 1, FWD_TI...  44.2 us

profile of v2, /device:TPU:0, one launch (start us, length us, event | category | flops | bytes accessed | tf_op | source)
XLA Modules:
  0.0 337.0 jit_solution(17343429583864351977)
XLA Ops:
  1.3 44.2 %forward.1 = (f32[3,2,4,1,512]{4,3,2,1,0:T(1,128)}, bf16[1024,2048]{1,0:T(8,128)(2,1)}, bf16[1024,2048]{1,0:T(8,128)(2,1)}, bf16[1024,2048]{1,0:T(8,128)(2,1)}, ...) custom-call(bf16[512,384]{1,0:T(8,128)(2,1)} %h_a.3, bf16[512,384]{1,0:T(8,128)(2,1)} %h_b.3, ...), custom_call_target="tpu_custom_call" | custom-call | tf_op jit(solution)/shard_map/forward/pallas_call | solution.py:581
  45.5 286.6 %main.1 = (f32[256,2048]{1,0:T(8,128)}, f32[256,2048]{1,0:T(8,128)}, f32[56,2048]{1,0:T(8,128)}) custom-call(bf16[1024,2048]{1,0:T(8,128)(2,1)} %get-tuple-element.26.zh_hbm, f32[2,4,512,512]{3,2,1,0:T(8,128)} %get-tuple-element.27.zn_hbm, bf16[1024,2048]{1,0:T(8,128)(2,1)} %get-tuple-element.28.x2_hbm, bf16[1024,2048]{1,0:T(8,128)(2,1)} %get-tuple-element.29.x1_hbm, ...), custom_call_target="tpu_custom_call" | custom-call | tf_op jit(solution)/shard_map/main/pallas_call | solution.py:594
  332.1 4.8 %finish.1 = (f32[48,2048]{1,0:T(8,128)}, f32[256,2048]{1,0:T(8,128)}, f32[256,2048]{1,0:T(8,128)}, f32[1,2048]{1,0:T(1,128)}, f32[1,2048]{1,0:T(1,128)}, /*index...) custom-call(f32[256,2048]{1,0:T(8,128)} %get-tuple-element.33.dw3_in, f32[256,2048]{1,0:T(8,128)} %get-tuple-element.34.dw2_in, ...), custom_call_target="tpu_custom_call" | custom-call | tf_op jit(solution)/shard_map/finish/pallas_call | solution.py:611

commit v3 on v2

--- a/solution.py
+++ b/solution.py
@@ -95,21 +95,30 @@
         st[i, 0, pl.ds(2 * v + 1, 1), :] = jnp.sum(weighted[part], axis=0, keepdims=True)
 
 
-def forward_kernel(h_a, h_b, w1_hbm, w2_hbm, w3_hbm, g1, b1, g2, b2,
+def copies_in(hbm, vmem, sem):
+    return [pltpu.make_async_copy(src, dst, sem.at[i]) for i, (src, dst) in enumerate(zip(hbm, vmem))]
+
+
+def forward_kernel(ha_hbm, hb_hbm, w1_hbm, w2_hbm, w3_hbm, g1_hbm, b1_hbm, g2_hbm, b2_hbm,
                    inv_out, x1_hbm, x2_hbm, zh_hbm, xh1_hbm, xh2_hbm, zn_hbm,
-                   x1, x2, zh, w1, wb, u, st, w1_sem, w_sem, norm_sem, act_sem, ssem, rsem):
+                   x1, x2, zh, w1, wb, u, st, h_a, h_b, g1, b1, g2, b2,
+                   w1_sem, w_sem, norm_sem, act_sem, ssem, rsem, in_sem):
     me = lax.axis_index("data")
+    inputs = copies_in((ha_hbm, hb_hbm, g1_hbm, b1_hbm, g2_hbm, b2_hbm), (h_a, h_b, g1, b1, g2, b2), in_sem)
     w1_copy = pltpu.make_async_copy(w1_hbm, w1, w1_sem)
     w1_copy.start()
+    for copy in inputs:
+        copy.start()
 
     def w_copy(layer):
         return pltpu.make_async_copy((w2_hbm, w3_hbm)[layer], wb.at[layer], w_sem.at[layer])
 
+    barrier_signal(me)
+    w1_copy.wait()
+    for copy in inputs:
+        copy.wait()
     for layer in range(2):
         w_copy(layer).start()
-    barrier_signal(me)
-    barrier_wait()
-    w1_copy.wait()
 
     acts = (x1, x2, zh)
     acts_hbm = (x1_hbm, x2_hbm, zh_hbm)
@@ -121,8 +130,9 @@
     def norm_copy(layer, v, q):
         return pltpu.make_async_copy(u.at[v, q], normed_hbm[layer].at[v, q], norm_sem.at[v, q])
 
-    def act_copy(layer, v):
-        return pltpu.make_async_copy(acts[layer].at[rows_of(v)], acts_hbm[layer].at[rows_of(v)], act_sem.at[layer, v])
+    def act_copy(layer, v, q):
+        return pltpu.make_async_copy(acts[layer].at[rows_of(v), fcols(q)], acts_hbm[layer].at[rows_of(v), fcols(q)],
+                                     act_sem.at[layer, v, q])
 
     def slot(layer, v, q):
         return (2 * layer + v) * FWD_TILES + q
@@ -156,18 +166,21 @@
                 u[v, q] = vals
                 st[slot(layer, v, q), 0, pl.ds(0, 1), :] = jnp.sum(vals, axis=0, keepdims=True)
                 st[slot(layer, v, q), 0, pl.ds(1, 1), :] = jnp.sum(vals * vals, axis=0, keepdims=True)
-                stats_send(me, st, ssem, rsem, slot(layer, v, q))
+                if matmul != (0, 0):
+                    stats_send(me, st, ssem, rsem, slot(layer, v, q))
             if norm is not None:
+                act_copy(n_layer, n_view, q).start()
                 norm_copy(n_layer, n_view, q).start()
             return carry
 
         if matmul in ((1, 0), (2, 0)):
             w_copy(matmul[0] - 1).wait()
         lax.fori_loop(0, FWD_TILES, body, 0)
-        if norm is not None:
-            act_copy(*norm).start()
 
     run(matmul=(0, 0))
+    barrier_wait()
+    for q in range(FWD_TILES):
+        stats_send(me, st, ssem, rsem, slot(0, 0, q))
     run(matmul=(0, 1))
     run(norm=(0, 0))
     run(matmul=(1, 0), norm=(0, 1))
@@ -178,8 +191,8 @@
     for v in range(2):
         for q in range(FWD_TILES):
             norm_copy(2, v, q).wait()
-        for layer in range(3):
-            act_copy(layer, v).wait()
+            for layer in range(3):
+                act_copy(layer, v, q).wait()
 
 
 class Ring:
@@ -281,13 +294,14 @@
 LAST_ROWS = LAST_COLS // TILE * PIECE
 FIRST_LAST = 3 * CHUNKS
 ITEMS = FIRST_LAST + LAST_ITEMS
-NORM_LAG = 4
+NORM_LAG = 2
 ST_LOSS = 4 * TILES
 
 
-def main_kernel(zh_hbm, zn_hbm, x2_hbm, x1_hbm, h_a, h_b, w3_hbm, w2_hbm, xh2_hbm, xh1_hbm,
-                inv, g1, b1, g2, b2, lam, dw3_hbm, dw2_hbm, small,
+def main_kernel(zh_hbm, zn_hbm, x2_hbm, x1_hbm, ha_hbm, hb_hbm, w3_hbm, w2_hbm, xh2_hbm, xh1_hbm,
+                inv_hbm, g1_hbm, b1_hbm, g2_hbm, b2_hbm, lam, dw3_hbm, dw2_hbm, small,
                 z, normed, acc, gt, gbuf, x2, x1, du2, ht, lt, wt, stage, loss_acc, st,
+                h_a, h_b, g1, b1, g2, b2, inv, in_sem,
                 z_sem, normed_sem, x_sem, w_sem, out_sem, ssem, rsem,
                 es, er, fs, fr, hs, hr, *ring_refs):
     me = lax.axis_index("data")
@@ -310,6 +324,10 @@
     barrier_wait()
     z_copy.wait()
     for copy in normed_copies(zn_hbm, normed_sem):
+        copy.start()
+    inputs = copies_in((ha_hbm, hb_hbm, g1_hbm, b1_hbm, g2_hbm, b2_hbm, inv_hbm),
+                       (h_a, h_b, g1, b1, g2, b2, inv), in_sem)
+    for copy in inputs:
         copy.start()
     x2_copy.start()
     x1_copy.start()
@@ -380,10 +398,13 @@
         stats_send(me, st, ssem, rsem, TILES + p)
 
     def corr_tick(p, carry):
-        for lag, work in ((0, corr_a), (LAG_C, both(ring.stage_c)), (LAG_D, both(corr_d)), (LAG_F, both(corr_f)),
-                          (LAG_H, both(corr_h)), (LAG_I, corr_i)):
+        last = PAIRS - 1
+        for lag, work, end in ((0, corr_a, last), (LAG_C, both(ring.stage_c), last), (LAG_D, both(corr_d), last),
+                               (LAG_F, both(corr_f), last), (LAG_I, corr_i, last - 2),
+                               (LAG_H, both(corr_h), last), (LAG_I, corr_i, last)):
             item = p - lag
-            pl.when((item >= 0) & (item < PAIRS))(functools.partial(work, item))
+            start = 0 if (lag, end) != (LAG_I, last) else last - 1
+            pl.when((item >= start) & (item <= end))(functools.partial(work, item))
         return carry
 
     st[:, 0] = jnp.zeros((st.shape[0],) + st.shape[2:], F32)
@@ -406,6 +427,8 @@
             z[rows, cols(q)] = (inv[2, v, q // 2, :, cols(q % 2)] * grad).astype(BF16)
         return carry
 
+    for copy in inputs:
+        copy.wait()
     out_norm(0, 0)
     x2_copy.wait()
 
@@ -432,30 +455,36 @@
             rows = e * TILE if isinstance(e, int) else pl.multiple_of(e * TILE, TILE)
             return pltpu.make_async_copy(w_hbm.at[pl.ds(rows, TILE), :], wt.at[e % 2], w_sem.at[e % 2])
 
-        def grad_tile(e, left=left, w_copy=w_copy, base=base, gain_ref=gain_ref, shift_ref=shift_ref):
-            w_copy(e).wait()
-            grad = dot_nt(left[...], wt[e % 2])
-            values = normed[e]
-            pre = gain_ref[:, cols(e)] * values + shift_ref[:, cols(e)]
-            grad = jnp.where(pre > 0, grad, 0.0)
-            gpre[e] = grad
-            stats_put(st, base + e, grad, grad * values)
-            stats_send(me, st, ssem, rsem, base + e)
-
-        def norm_tile(e, g=g, base=base, grad_out=grad_out, gain_ref=gain_ref):
-            stats_wait(st, ssem, rsem, base + e)
-            total = stats_total(st, base + e)
-            for k in range(2):
-                small[pl.ds(PIECE + 2 * g + k, 1), cols(e)] = total[k:k + 1] + total[k + 2:k + 3]
-            total = total * (1.0 / TOTAL_ROWS)
-            for v in range(2):
-                rows = pl.ds(v * VIEW, VIEW)
-                grad = gpre[e, rows, :] - (
-                    total[2 * v:2 * v + 1] + normed[e, rows, :] * total[2 * v + 1:2 * v + 2])
-                scale = gain_ref[:, cols(e)] * inv[1 - g, v, e // 2, :, cols(e % 2)]
-                grad_out[rows, cols(e)] = (scale * grad).astype(BF16)
-
-        def tick(q, carry, g=g, left=left, right=right, grad_tile=grad_tile, norm_tile=norm_tile, w_copy=w_copy,
+        def grad_step(e, grad, norm, g=g, left=left, w_copy=w_copy, base=base, grad_out=grad_out,
+                      gain_ref=gain_ref, shift_ref=shift_ref):
+            d = e - NORM_LAG
+            if grad:
+                w_copy(e).wait()
+            if norm:
+                stats_wait(st, ssem, rsem, base + d)
+            if grad:
+                vals = dot_nt(left[...], wt[e % 2])
+            if norm:
+                total = stats_total(st, base + d)
+                for k in range(2):
+                    small[pl.ds(PIECE + 2 * g + k, 1), cols(d)] = total[k:k + 1] + total[k + 2:k + 3]
+                total = total * (1.0 / TOTAL_ROWS)
+                for v in range(2):
+                    rows = pl.ds(v * VIEW, VIEW)
+                    out = gpre[d, rows, :] - (
+                        total[2 * v:2 * v + 1] + normed[d, rows, :] * total[2 * v + 1:2 * v + 2])
+                    scale = gain_ref[:, cols(d)] * inv[1 - g, v, d // 2, :, cols(d % 2)]
+                    grad_out[rows, cols(d)] = (scale * out).astype(BF16)
+            if grad:
+                values = normed[e]
+                pre = gain_ref[:, cols(e)] * values + shift_ref[:, cols(e)]
+                vals = jnp.where(pre > 0, vals, 0.0)
+                gpre[e] = vals
+                stats_put(st, base + e, vals, vals * values)
+                stats_send(me, st, ssem, rsem, base + e)
+                pl.when(e + 2 < TILES)(lambda: w_copy(e + 2).start())
+
+        def tick(q, carry, g=g, left=left, right=right, grad_step=grad_step, w_copy=w_copy,
                  xh_hbm=xh_hbm):
             p = (1 + g) * PAIRS + q
             lt[...] = left[:, cols(q)].T
@@ -476,16 +505,15 @@
                 for copy in normed_copies(xh_hbm, normed_sem):
                     copy.wait()
 
-            def step(k, carry):
-                e = 2 * (q - 1) + k
-                pl.when(e < TILES)(lambda: grad_tile(e))
-                pl.when((e >= NORM_LAG) & (e < TILES + NORM_LAG))(lambda: norm_tile(e - NORM_LAG))
-                pl.when(e + 2 < TILES)(lambda: w_copy(e + 2).start())
+            def step(e, carry):
+                pl.when(e < NORM_LAG)(lambda: grad_step(e, True, False))
+                pl.when((e >= NORM_LAG) & (e < TILES))(lambda: grad_step(e, True, True))
+                pl.when(e >= TILES)(lambda: grad_step(e, False, True))
                 return carry
 
             @pl.when(q >= 1)
             def _():
-                lax.fori_loop(0, 2, step, 0)
+                lax.fori_loop((q - 1) * 3 // 2, q * 3 // 2, step, 0)
 
             if g == 0:
                 pl.when(q > 0)(lambda: both(ring.stage_b)(p))
@@ -541,9 +569,9 @@
     loads = [pltpu.make_async_copy(small_in, vs, in_sem.at[0])]
     stores = [pltpu.make_async_copy(vs.at[pl.ds(0, PIECE)], dw1, out_sem.at[0])]
     for k, (src, mid, dst) in enumerate(((dw3_in, v3, dw3), (dw2_in, v2, dw2))):
-        for part in range(4):
-            rows = pl.ds(part * TILE // 4, TILE // 4)
-            i = 1 + 4 * k + part
+        for part in range(2):
+            rows = pl.ds(part * TILE // 2, TILE // 2)
+            i = 1 + 2 * k + part
             loads.append(pltpu.make_async_copy(src.at[rows], mid.at[rows], in_sem.at[i]))
             stores.append(pltpu.make_async_copy(mid.at[rows], dst.at[rows], out_sem.at[i]))
     for load in loads:
@@ -552,7 +580,8 @@
         load.wait()
         store.start()
     for k, ref in enumerate((gs2, gg2, gs1, gg1)):
-        ref[...] = vs[pl.ds(PIECE + k, 1), :]
+        stores.append(pltpu.make_async_copy(vs.at[pl.ds(PIECE + k, 1), :], ref, out_sem.at[5 + k]))
+        stores[-1].start()
     loss[...] = vs[pl.ds(PIECE + 4, 1), pl.ds(0, 1)]
     for store in stores:
         store.wait()
@@ -575,26 +604,29 @@
     weight = sds((TILE, WIDTH), F32)
     vector = sds((1, WIDTH), F32)
     small = 2 * PIECE - 40
+    small_inputs = [pltpu.VMEM((VIEW, FEAT), BF16)] * 2 + [pltpu.VMEM((1, WIDTH), F32)] * 4
 
     def local_step(h_a, h_b, w_one, w_two, w_three, gain_one, shift_one, gain_two, shift_two, lam_off):
         g1, b1, g2, b2 = (v.reshape(1, WIDTH) for v in (gain_one, shift_one, gain_two, shift_two))
         inv, x1, x2, zh, xh1, xh2, zn = pl.pallas_call(
             forward_kernel,
             out_shape=(sds((3, 2, FWD_TILES, 1, FWD_TILE), F32), act, act, act, normed, normed, normed),
-            in_specs=[VMEM_SPEC] * 2 + [ANY_SPEC] * 3 + [VMEM_SPEC] * 4,
+            in_specs=[ANY_SPEC] * 9,
             out_specs=(VMEM_SPEC,) + (ANY_SPEC,) * 6,
             scratch_shapes=[
                 pltpu.VMEM((ROWS, WIDTH), BF16), pltpu.VMEM((ROWS, WIDTH), BF16), pltpu.VMEM((ROWS, WIDTH), BF16),
                 pltpu.VMEM((FEAT, WIDTH), BF16), pltpu.VMEM((2, WIDTH, WIDTH), BF16),
                 pltpu.VMEM((2, FWD_TILES, VIEW, FWD_TILE), F32), pltpu.VMEM((6 * FWD_TILES, 8, 2, FWD_TILE), F32),
-                DMA, DMA((2,)), DMA((2, FWD_TILES)), DMA((3, 2)), DMA((6 * FWD_TILES,)), DMA((6 * FWD_TILES,)),
+            ] + small_inputs + [
+                DMA, DMA((2,)), DMA((2, FWD_TILES)), DMA((3, 2, FWD_TILES)), DMA((6 * FWD_TILES,)), DMA((6 * FWD_TILES,)),
+                DMA((6,)),
             ],
             compiler_params=params(0), name="forward",
         )(h_a, h_b, w_one, w_two, w_three, g1, b1, g2, b2)
         dw3, dw2, rest = pl.pallas_call(
             main_kernel,
             out_shape=(weight, weight, sds((small, WIDTH), F32)),
-            in_specs=[ANY_SPEC] * 4 + [VMEM_SPEC] * 2 + [ANY_SPEC] * 4 + [VMEM_SPEC] * 5 + [SMEM_SPEC],
+            in_specs=[ANY_SPEC] * 15 + [SMEM_SPEC],
             out_specs=(ANY_SPEC, ANY_SPEC, VMEM_SPEC),
             scratch_shapes=[
                 pltpu.VMEM((ROWS, WIDTH), BF16), pltpu.VMEM((TILES, ROWS, TILE), F32),
@@ -604,7 +636,8 @@
                 pltpu.VMEM((FEAT, ROWS), BF16), pltpu.VMEM((TILE, ROWS), BF16),
                 pltpu.VMEM((2, TILE, WIDTH), BF16), pltpu.VMEM((2, TILE, CHUNK), F32),
                 pltpu.VMEM((1, TILE), F32), pltpu.VMEM((ST_LOSS + 1, 8, 4, TILE), F32),
-                DMA, DMA((2, TILES)), DMA((2,)), DMA((2,)), DMA((2,)), DMA((ST_LOSS + 1,)), DMA((ST_LOSS + 1,)),
+            ] + small_inputs + [
+                pltpu.VMEM((3, 2, FWD_TILES, 1, FWD_TILE), F32), DMA((7,)), DMA, DMA((2, TILES)), DMA((2,)), DMA((2,)), DMA((2,)), DMA((ST_LOSS + 1,)), DMA((ST_LOSS + 1,)),
             ] + [DMA((CHUNKS,))] * 6 + RING_SCRATCH,
             compiler_params=params(1), name="main",
         )(zh, zn, x2, x1, h_a, h_b, w_three, w_two, xh2, xh1, inv, g1, b1, g2, b2, lam_off.reshape(1, 1))
@@ -612,10 +645,10 @@
             finish_kernel,
             out_shape=(sds((PIECE, WIDTH), F32), weight, weight, vector, vector, vector, vector, sds((1, 1), F32)),
             in_specs=[ANY_SPEC] * 3,
-            out_specs=(ANY_SPEC,) * 3 + (VMEM_SPEC,) * 5,
+            out_specs=(ANY_SPEC,) * 7 + (VMEM_SPEC,),
             scratch_shapes=[
                 pltpu.VMEM((TILE, WIDTH), F32), pltpu.VMEM((TILE, WIDTH), F32), pltpu.VMEM((small, WIDTH), F32),
-                DMA((9,)), DMA((9,)),
+                DMA((5,)), DMA((9,)),
             ],
             compiler_params=pltpu.CompilerParams(vmem_limit_bytes=66_000_000), name="finish",
         )(dw3, dw2, rest)

time: 337 us -> 331 us (0.982)
  Pallas kernels: 336 us -> 329 us
where the time goes in v3:
time: 331 us
  Pallas kernels  329 us (99%)
    pallas_call x1, Pallas kernels, local_step(): pl.pallas_call(main_kernel, out_shape=(weight, weight, sds((small, WIDTH)...  284 us
    pallas_call x1, Pallas kernels, local_step(): pl.pallas_call(forward_kernel, out_shape=(sds((3, 2, FWD_TILES, 1, FWD_TI...  41.1 us

profile of v3, /device:TPU:0, one launch (start us, length us, event | category | flops | bytes accessed | tf_op | source)
XLA Modules:
  0.0 330.5 jit_solution(14274282037518875210)
XLA Ops:
  1.3 41.1 %forward.1 = (f32[3,2,4,1,512]{4,3,2,1,0:T(1,128)}, bf16[1024,2048]{1,0:T(8,128)(2,1)}, bf16[1024,2048]{1,0:T(8,128)(2,1)}, bf16[1024,2048]{1,0:T(8,128)(2,1)}, ...) custom-call(bf16[512,384]{1,0:T(8,128)(2,1)} %ha_hbm.3, ...), custom_call_target="tpu_custom_call" | custom-call | tf_op jit(solution)/shard_map/forward/pallas_call | solution.py:611
  42.4 283.5 %main.1 = (f32[256,2048]{1,0:T(8,128)}, f32[256,2048]{1,0:T(8,128)}, f32[56,2048]{1,0:T(8,128)}) custom-call(bf16[1024,2048]{1,0:T(8,128)(2,1)} %get-tuple-element.26.zh_hbm, f32[2,4,512,512]{3,2,1,0:T(8,128)} %get-tuple-element.27.zn_hbm, bf16[1024,2048]{1,0:T(8,128)(2,1)} %get-tuple-element.28.x2_hbm, bf16[1024,2048]{1,0:T(8,128)(2,1)} %get-tuple-element.29.x1_hbm, ...), custom_call_target="tpu_custom_call" | custom-call | tf_op jit(solution)/shard_map/main/pallas_call | solution.py:626
  325.9 4.4 %finish.1 = (f32[48,2048]{1,0:T(8,128)}, f32[256,2048]{1,0:T(8,128)}, f32[256,2048]{1,0:T(8,128)}, f32[1,2048]{1,0:T(1,128)}, f32[1,2048]{1,0:T(1,128)}, /*index...) custom-call(f32[256,2048]{1,0:T(8,128)} %get-tuple-element.33.dw3_in, f32[256,2048]{1,0:T(8,128)} %get-tuple-element.34.dw2_in, ...), custom_call_target="tpu_custom_call" | custom-call | tf_op jit(solution)/shard_map/finish/pallas_call | solution.py:644

commit v4 on v3

--- a/solution.py
+++ b/solution.py
@@ -19,12 +19,14 @@
 TILES = WIDTH // TILE
 FWD_TILE = 512
 FWD_TILES = WIDTH // FWD_TILE
+RATIO = FWD_TILE // TILE
 PIECE = FEAT // 8
 CHUNK = 128
 CHUNKS = WIDTH // CHUNK
-PAIRS = CHUNKS // 2
+PER = TILE // CHUNK
+PAIRS = CHUNKS // PER
 LAG_C, LAG_D, LAG_F, LAG_H, LAG_I = 1, 2, 3, 4, 5
-PA_SLOTS, R0_SLOTS, R1_SLOTS, R2_SLOTS = 6, 2, 4, 4
+PA_SLOTS, R0_SLOTS, R1_SLOTS, R2_SLOTS = 3 * PER, PER, 2 * PER, 2 * PER
 
 
 def dot_nn(a, b):
@@ -100,8 +102,8 @@
 
 
 def forward_kernel(ha_hbm, hb_hbm, w1_hbm, w2_hbm, w3_hbm, g1_hbm, b1_hbm, g2_hbm, b2_hbm,
-                   inv_out, x1_hbm, x2_hbm, zh_hbm, xh1_hbm, xh2_hbm, zn_hbm,
-                   x1, x2, zh, w1, wb, u, st, h_a, h_b, g1, b1, g2, b2,
+                   inv_hbm, x1_hbm, x2_hbm, zh_hbm, xh1_hbm, xh2_hbm, zn_hbm,
+                   x1, x2, zh, w1, wb, u, st, h_a, h_b, g1, b1, g2, b2, inv_out, inv_sem,
                    w1_sem, w_sem, norm_sem, act_sem, ssem, rsem, in_sem):
     me = lax.axis_index("data")
     inputs = copies_in((ha_hbm, hb_hbm, g1_hbm, b1_hbm, g2_hbm, b2_hbm), (h_a, h_b, g1, b1, g2, b2), in_sem)
@@ -133,6 +135,9 @@
     def act_copy(layer, v, q):
         return pltpu.make_async_copy(acts[layer].at[rows_of(v), fcols(q)], acts_hbm[layer].at[rows_of(v), fcols(q)],
                                      act_sem.at[layer, v, q])
+
+    def inv_copy(layer, v):
+        return pltpu.make_async_copy(inv_out.at[layer, v], inv_hbm.at[layer, v], inv_sem.at[layer, v])
 
     def slot(layer, v, q):
         return (2 * layer + v) * FWD_TILES + q
@@ -176,6 +181,8 @@
         if matmul in ((1, 0), (2, 0)):
             w_copy(matmul[0] - 1).wait()
         lax.fori_loop(0, FWD_TILES, body, 0)
+        if norm is not None:
+            inv_copy(*norm).start()
 
     run(matmul=(0, 0))
     barrier_wait()
@@ -189,6 +196,8 @@
     run(matmul=(2, 1), norm=(2, 0))
     run(norm=(2, 1))
     for v in range(2):
+        for layer in range(3):
+            inv_copy(layer, v).wait()
         for q in range(FWD_TILES):
             norm_copy(2, v, q).wait()
             for layer in range(3):
@@ -271,10 +280,12 @@
             x, y = chip % 2, chip // 2
             for c in range(2):
                 a, b = (y, x) if c else (x, y)
-                for k in range(2):
-                    self.pa[(2 * p + k) % PA_SLOTS, c, a, b] = part[k * CHUNK:(k + 1) * CHUNK, c * TILE:(c + 1) * TILE]
-        self.send0(2 * p)
-        self.send0(2 * p + 1)
+                for k in range(PER):
+                    self.pa[(PER * p + k) % PA_SLOTS, c, a, b] = part[k * CHUNK:(k + 1) * CHUNK, c * TILE:(c + 1) * TILE]
+
+    def send_tick(self, p):
+        for k in range(PER):
+            self.send0(PER * p + k)
 
 
 RING_SCRATCH = [
@@ -289,7 +300,7 @@
 ]
 
 
-LAST_COLS = 512
+LAST_COLS = 1024 // PER
 LAST_ITEMS = WIDTH // LAST_COLS
 LAST_ROWS = LAST_COLS // TILE * PIECE
 FIRST_LAST = 3 * CHUNKS
@@ -299,9 +310,9 @@
 
 
 def main_kernel(zh_hbm, zn_hbm, x2_hbm, x1_hbm, ha_hbm, hb_hbm, w3_hbm, w2_hbm, xh2_hbm, xh1_hbm,
-                inv_hbm, g1_hbm, b1_hbm, g2_hbm, b2_hbm, lam, dw3_hbm, dw2_hbm, small,
+                inv_hbm, g1_hbm, b1_hbm, g2_hbm, b2_hbm, lam, dw3_hbm, dw2_hbm, small_hbm,
                 z, normed, acc, gt, gbuf, x2, x1, du2, ht, lt, wt, stage, loss_acc, st,
-                h_a, h_b, g1, b1, g2, b2, inv, in_sem,
+                h_a, h_b, g1, b1, g2, b2, inv, small, small_sem, in_sem,
                 z_sem, normed_sem, x_sem, w_sem, out_sem, ssem, rsem,
                 es, er, fs, fr, hs, hr, *ring_refs):
     me = lax.axis_index("data")
@@ -311,7 +322,7 @@
 
     def normed_copies(src, sem):
         return [pltpu.make_async_copy(
-            src.at[v, q // 2, :, cols(q % 2)], normed.at[q, pl.ds(v * VIEW, VIEW)], sem.at[v, q])
+            src.at[v, q // RATIO, :, cols(q % RATIO)], normed.at[q, pl.ds(v * VIEW, VIEW)], sem.at[v, q])
             for v in range(2) for q in range(TILES)]
 
     z_copy.start()
@@ -319,9 +330,6 @@
     ring = Ring(me, ITEMS, *ring_refs[:4], ring_refs[4:10], ring_refs[10:])
     core, f, s = ring.core, ring.f, ring.s
     lam_val = lam[0, 0]
-    acc[...] = jnp.zeros_like(acc)
-    loss_acc[...] = jnp.zeros_like(loss_acc)
-    barrier_wait()
     z_copy.wait()
     for copy in normed_copies(zn_hbm, normed_sem):
         copy.start()
@@ -345,16 +353,23 @@
         block = gt.at[t, core]
         return ring.copy(block, block, hs.at[t], hr.at[t], ring.partner)
 
-    def both(work):
+    def each(work):
         def run(p):
-            work(2 * p)
-            work(2 * p + 1)
+            for k in range(PER):
+                work(PER * p + k)
         return run
 
-    def corr_a(p):
+    def corr_partial(p):
         lt[:, view_a] = z[view_b, cols(p)].T
         ring.partial(p, lt[:, view_a], z.at[view_a])
-        both(ring.stage_b)(p)
+
+    def corr_send(p):
+        ring.send_tick(p)
+        each(ring.stage_b)(p)
+
+    def corr_a(p):
+        corr_partial(p)
+        corr_send(p)
 
     def corr_d(t):
         corr = ring.stage_d(t) * (1.0 / TOTAL_ROWS)
@@ -375,12 +390,12 @@
         copy_h(t).start()
 
     def corr_i(p):
-        both(lambda t: copy_h(t).wait())(p)
+        each(lambda t: copy_h(t).wait())(p)
         for dev in range(8):
             c, x, y = dev % 2, (dev // 2) % 2, dev // 4
             a, b = (y, x) if c else (x, y)
-            for k in range(2):
-                gbuf[pl.ds(k * CHUNK, CHUNK), cols(dev)] = gt[2 * p + k, c, a, b]
+            for k in range(PER):
+                gbuf[pl.ds(k * CHUNK, CHUNK), cols(dev)] = gt[PER * p + k, c, a, b]
         grad_b = dot_nt(z[view_a, :], gbuf[...])
         acc[p, view_b, :] = grad_b
         for k in range(4):
@@ -399,16 +414,21 @@
 
     def corr_tick(p, carry):
         last = PAIRS - 1
-        for lag, work, end in ((0, corr_a, last), (LAG_C, both(ring.stage_c), last), (LAG_D, both(corr_d), last),
-                               (LAG_F, both(corr_f), last), (LAG_I, corr_i, last - 2),
-                               (LAG_H, both(corr_h), last), (LAG_I, corr_i, last)):
+        for lag, work, end in ((0, corr_a, last), (LAG_C, each(ring.stage_c), last), (LAG_D, each(corr_d), last),
+                               (LAG_F, each(corr_f), last), (LAG_I, corr_i, last - 2),
+                               (LAG_H, each(corr_h), last), (LAG_I, corr_i, last)):
             item = p - lag
-            start = 0 if (lag, end) != (LAG_I, last) else last - 1
+            start = {0: 1, LAG_I: 0 if end < last else last - 1}.get(lag, 0)
             pl.when((item >= start) & (item <= end))(functools.partial(work, item))
         return carry
 
+    corr_partial(0)
+    barrier_wait()
+    corr_send(0)
+    acc[...] = jnp.zeros_like(acc)
+    loss_acc[...] = jnp.zeros_like(loss_acc)
     st[:, 0] = jnp.zeros((st.shape[0],) + st.shape[2:], F32)
-    lax.fori_loop(0, PAIRS + LAG_I, corr_tick, 0)
+    lax.fori_loop(1, PAIRS + LAG_I, corr_tick, 0)
 
     def out_sums(q, carry):
         grad = acc[q, view_a, :]
@@ -424,7 +444,7 @@
             total = stats_total(st, v * TILES + q) * (1.0 / TOTAL_ROWS)
             rows = pl.ds(v * VIEW, VIEW)
             grad = acc[q, rows, :] - (total[0:1] + normed[q, rows, :] * total[1:2])
-            z[rows, cols(q)] = (inv[2, v, q // 2, :, cols(q % 2)] * grad).astype(BF16)
+            z[rows, cols(q)] = (inv[2, v, q // RATIO, :, cols(q % RATIO)] * grad).astype(BF16)
         return carry
 
     for copy in inputs:
@@ -473,7 +493,7 @@
                     rows = pl.ds(v * VIEW, VIEW)
                     out = gpre[d, rows, :] - (
                         total[2 * v:2 * v + 1] + normed[d, rows, :] * total[2 * v + 1:2 * v + 2])
-                    scale = gain_ref[:, cols(d)] * inv[1 - g, v, d // 2, :, cols(d % 2)]
+                    scale = gain_ref[:, cols(d)] * inv[1 - g, v, d // RATIO, :, cols(d % RATIO)]
                     grad_out[rows, cols(d)] = (scale * out).astype(BF16)
             if grad:
                 values = normed[e]
@@ -489,11 +509,12 @@
             p = (1 + g) * PAIRS + q
             lt[...] = left[:, cols(q)].T
             ring.partial(p, lt[...], right)
+            ring.send_tick(p)
+            each(ring.stage_b)(p)
 
             @pl.when(q == 0)
             def _():
                 if g == 0:
-                    both(ring.stage_b)(p)
                     lax.fori_loop(1, TILES, out_norm, 0)
                 w_copy(0).start()
                 w_copy(1).start()
@@ -516,13 +537,11 @@
                 lax.fori_loop((q - 1) * 3 // 2, q * 3 // 2, step, 0)
 
             if g == 0:
-                pl.when(q > 0)(lambda: both(ring.stage_b)(p))
-                pl.when(q >= LAG_C)(lambda: both(ring.stage_c)(p - LAG_C))
-                pl.when(q >= LAG_D)(lambda: both(store_out)(p - LAG_D))
+                pl.when(q >= LAG_C)(lambda: each(ring.stage_c)(p - LAG_C))
+                pl.when(q >= LAG_D)(lambda: each(store_out)(p - LAG_D))
             else:
-                both(ring.stage_b)(p)
-                both(ring.stage_c)(p - LAG_C)
-                both(store_out)(p - LAG_D)
+                each(ring.stage_c)(p - LAG_C)
+                each(store_out)(p - LAG_D)
             return carry
 
         if g == 1:
@@ -536,7 +555,13 @@
     def rows_of(t):
         return LAST_ROWS if t >= FIRST_LAST else CHUNK
 
-    for t in range(FIRST_LAST, ITEMS + 2 * LAG_D):
+    def part_copy(k):
+        block = (pl.ds(0, PIECE), pl.ds(k * LAST_COLS, LAST_COLS))
+        return pltpu.make_async_copy(small.at[block], small_hbm.at[block], small_sem.at[k])
+
+    sums_rows = (pl.ds(PIECE, 8), slice(None))
+    sums_copy = pltpu.make_async_copy(small.at[sums_rows], small_hbm.at[sums_rows], small_sem.at[LAST_ITEMS])
+    for t in range(FIRST_LAST, ITEMS + PER * LAG_D):
         if t < ITEMS:
             for m in range(per_item):
                 part = dot_nn(ht[...], z[:, cols((t - FIRST_LAST) * per_item + m)])
@@ -546,23 +571,29 @@
                     ring.pa[t % PA_SLOTS, c, a, b, m * PIECE:(m + 1) * PIECE] = part[dev * PIECE:(dev + 1) * PIECE]
             ring.send0(t, LAST_ROWS)
             ring.stage_b(t, LAST_ROWS)
-        if t - 2 * LAG_C < ITEMS:
-            ring.stage_c(t - 2 * LAG_C, rows_of(t - 2 * LAG_C))
-        d = t - 2 * LAG_D
+        if t - PER * LAG_C < ITEMS:
+            ring.stage_c(t - PER * LAG_C, rows_of(t - PER * LAG_C))
+        d = t - PER * LAG_D
         if d < FIRST_LAST:
             store_out(d)
         else:
             total = ring.stage_d(d, LAST_ROWS)
             for m in range(per_item):
                 small[pl.ds(0, PIECE), cols((d - FIRST_LAST) * per_item + m)] = total[m * PIECE:(m + 1) * PIECE]
+            part_copy(d - FIRST_LAST).start()
+        if t == FIRST_LAST + 4:
+            stats_wait(st, ssem, rsem, ST_LOSS)
+            loss = jnp.sum(stats_total(st, ST_LOSS), keepdims=True)
+            small[pl.ds(PIECE + 4, 4), :] = jnp.broadcast_to(loss, (4, WIDTH))
+            sums_copy.start()
         if t == FIRST_LAST:
             st[ST_LOSS, 0, pl.ds(0, 1), :] = loss_acc[...]
             stats_send(me, st, ssem, rsem, ST_LOSS)
     for t in (FIRST_LAST - 2, FIRST_LAST - 1):
         out_copy(t, dw2_hbm).wait()
-    stats_wait(st, ssem, rsem, ST_LOSS)
-    loss = jnp.sum(stats_total(st, ST_LOSS), keepdims=True)
-    small[pl.ds(PIECE + 4, 4), :] = jnp.broadcast_to(loss, (4, WIDTH))
+    sums_copy.wait()
+    for k in range(LAST_ITEMS):
+        part_copy(k).wait()
 
 
 def finish_kernel(dw3_in, dw2_in, small_in, dw1, dw2, dw3, gg1, gs1, gg2, gs2, loss, v3, v2, vs, in_sem, out_sem):
@@ -612,12 +643,13 @@
             forward_kernel,
             out_shape=(sds((3, 2, FWD_TILES, 1, FWD_TILE), F32), act, act, act, normed, normed, normed),
             in_specs=[ANY_SPEC] * 9,
-            out_specs=(VMEM_SPEC,) + (ANY_SPEC,) * 6,
+            out_specs=(ANY_SPEC,) * 7,
             scratch_shapes=[
                 pltpu.VMEM((ROWS, WIDTH), BF16), pltpu.VMEM((ROWS, WIDTH), BF16), pltpu.VMEM((ROWS, WIDTH), BF16),
                 pltpu.VMEM((FEAT, WIDTH), BF16), pltpu.VMEM((2, WIDTH, WIDTH), BF16),
                 pltpu.VMEM((2, FWD_TILES, VIEW, FWD_TILE), F32), pltpu.VMEM((6 * FWD_TILES, 8, 2, FWD_TILE), F32),
             ] + small_inputs + [
+                pltpu.VMEM((3, 2, FWD_TILES, 1, FWD_TILE), F32), DMA((3, 2)),
                 DMA, DMA((2,)), DMA((2, FWD_TILES)), DMA((3, 2, FWD_TILES)), DMA((6 * FWD_TILES,)), DMA((6 * FWD_TILES,)),
                 DMA((6,)),
             ],
@@ -627,7 +659,7 @@
             main_kernel,
             out_shape=(weight, weight, sds((small, WIDTH), F32)),
             in_specs=[ANY_SPEC] * 15 + [SMEM_SPEC],
-            out_specs=(ANY_SPEC, ANY_SPEC, VMEM_SPEC),
+            out_specs=(ANY_SPEC,) * 3,
             scratch_shapes=[
                 pltpu.VMEM((ROWS, WIDTH), BF16), pltpu.VMEM((TILES, ROWS, TILE), F32),
                 pltpu.VMEM((TILES, ROWS, TILE), F32), pltpu.VMEM((CHUNKS, 2, 2, 2, CHUNK, TILE), BF16),
@@ -637,7 +669,8 @@
                 pltpu.VMEM((2, TILE, WIDTH), BF16), pltpu.VMEM((2, TILE, CHUNK), F32),
                 pltpu.VMEM((1, TILE), F32), pltpu.VMEM((ST_LOSS + 1, 8, 4, TILE), F32),
             ] + small_inputs + [
-                pltpu.VMEM((3, 2, FWD_TILES, 1, FWD_TILE), F32), DMA((7,)), DMA, DMA((2, TILES)), DMA((2,)), DMA((2,)), DMA((2,)), DMA((ST_LOSS + 1,)), DMA((ST_LOSS + 1,)),
+                pltpu.VMEM((3, 2, FWD_TILES, 1, FWD_TILE), F32),
+                pltpu.VMEM((small, WIDTH), F32), DMA((LAST_ITEMS + 1,)), DMA((7,)), DMA, DMA((2, TILES)), DMA((2,)), DMA((2,)), DMA((2,)), DMA((ST_LOSS + 1,)), DMA((ST_LOSS + 1,)),
             ] + [DMA((CHUNKS,))] * 6 + RING_SCRATCH,
             compiler_params=params(1), name="main",
         )(zh, zn, x2, x1, h_a, h_b, w_three, w_two, xh2, xh1, inv, g1, b1, g2, b2, lam_off.reshape(1, 1))

time: 331 us -> 329 us (level)
  no operation moved by 1% of the time
where the time goes in v4:
time: 329 us
  Pallas kernels  327 us (99%)
    pallas_call x1, Pallas kernels, local_step(): pl.pallas_call(main_kernel, out_shape=(weight, weight, sds((small, WIDTH)...  282 us
    pallas_call x1, Pallas kernels, local_step(): pl.pallas_call(forward_kernel, out_shape=(sds((3, 2, FWD_TILES, 1, FWD_TI...  40.6 us

profile of v4, /device:TPU:0, one launch (start us, length us, event | category | flops | bytes accessed | tf_op | source)
XLA Modules:
  0.0 328.8 jit_solution(10719300665267446760)
XLA Ops:
  1.3 40.6 %forward.1 = (f32[3,2,4,1,512]{4,3,2,1,0:T(1,128)}, bf16[1024,2048]{1,0:T(8,128)(2,1)}, bf16[1024,2048]{1,0:T(8,128)(2,1)}, bf16[1024,2048]{1,0:T(8,128)(2,1)}, ...) custom-call(bf16[512,384]{1,0:T(8,128)(2,1)} %ha_hbm.3, ...), custom_call_target="tpu_custom_call" | custom-call | tf_op jit(solution)/shard_map/forward/pallas_call | solution.py:642
  41.9 282.2 %main.1 = (f32[256,2048]{1,0:T(8,128)}, f32[256,2048]{1,0:T(8,128)}, f32[56,2048]{1,0:T(8,128)}) custom-call(bf16[1024,2048]{1,0:T(8,128)(2,1)} %get-tuple-element.26.zh_hbm, f32[2,4,512,512]{3,2,1,0:T(8,128)} %get-tuple-element.27.zn_hbm, bf16[1024,2048]{1,0:T(8,128)(2,1)} %get-tuple-element.28.x2_hbm, bf16[1024,2048]{1,0:T(8,128)(2,1)} %get-tuple-element.29.x1_hbm, ...), custom_call_target="tpu_custom_call" | custom-call | tf_op jit(solution)/shard_map/main/pallas_call | solution.py:658
  324.1 4.4 %finish.1 = (f32[48,2048]{1,0:T(8,128)}, f32[256,2048]{1,0:T(8,128)}, f32[256,2048]{1,0:T(8,128)}, f32[1,2048]{1,0:T(1,128)}, f32[1,2048]{1,0:T(1,128)}, /*index...) custom-call(f32[256,2048]{1,0:T(8,128)} %get-tuple-element.33.dw3_in, f32[256,2048]{1,0:T(8,128)} %get-tuple-element.34.dw2_in, ...), custom_call_target="tpu_custom_call" | custom-call | tf_op jit(solution)/shard_map/finish/pallas_call | solution.py:677

commit v5 on v4

--- a/solution.py
+++ b/solution.py
@@ -310,10 +310,10 @@
 
 
 def main_kernel(zh_hbm, zn_hbm, x2_hbm, x1_hbm, ha_hbm, hb_hbm, w3_hbm, w2_hbm, xh2_hbm, xh1_hbm,
-                inv_hbm, g1_hbm, b1_hbm, g2_hbm, b2_hbm, lam, dw3_hbm, dw2_hbm, small_hbm,
-                z, normed, acc, gt, gbuf, x2, x1, du2, ht, lt, wt, stage, loss_acc, st,
-                h_a, h_b, g1, b1, g2, b2, inv, small, small_sem, in_sem,
-                z_sem, normed_sem, x_sem, w_sem, out_sem, ssem, rsem,
+                inv_hbm, g1_hbm, b1_hbm, g2_hbm, b2_hbm, lam, dw3, dw2, small,
+                z, normed, acc, gt, gbuf, x2, x1, du2, ht, lt, wt, loss_acc, st,
+                h_a, h_b, g1, b1, g2, b2, inv, in_sem,
+                z_sem, normed_sem, x_sem, w_sem, ssem, rsem,
                 es, er, fs, fr, hs, hr, *ring_refs):
     me = lax.axis_index("data")
     z_copy = pltpu.make_async_copy(zh_hbm, z, z_sem)
@@ -452,17 +452,17 @@
     out_norm(0, 0)
     x2_copy.wait()
 
-    def out_copy(t, hbm):
-        return pltpu.make_async_copy(stage.at[t % 2], hbm.at[:, cols(t % CHUNKS, CHUNK)], out_sem.at[t % 2])
-
     def store_out(t):
-        when_in(t >= CHUNKS + 2, lambda: out_copy(t - 2, dw3_hbm).wait())
-        stage[t % 2] = ring.stage_d(t).T
-        if isinstance(t, int):
-            out_copy(t, dw2_hbm if t >= 2 * CHUNKS else dw3_hbm).start()
-        else:
-            pl.when(t < 2 * CHUNKS)(lambda: out_copy(t, dw3_hbm).start())
-            pl.when(t >= 2 * CHUNKS)(lambda: out_copy(t, dw2_hbm).start())
+        block = ring.stage_d(t).T
+
+        def third():
+            dw3[:, cols(t % CHUNKS, CHUNK)] = block
+
+        def second():
+            dw2[:, cols(t % CHUNKS, CHUNK)] = block
+
+        when_in(t < 2 * CHUNKS, third)
+        when_in(t >= 2 * CHUNKS, second)
 
     gpre = acc
     for g in range(2):
@@ -555,12 +555,6 @@
     def rows_of(t):
         return LAST_ROWS if t >= FIRST_LAST else CHUNK
 
-    def part_copy(k):
-        block = (pl.ds(0, PIECE), pl.ds(k * LAST_COLS, LAST_COLS))
-        return pltpu.make_async_copy(small.at[block], small_hbm.at[block], small_sem.at[k])
-
-    sums_rows = (pl.ds(PIECE, 8), slice(None))
-    sums_copy = pltpu.make_async_copy(small.at[sums_rows], small_hbm.at[sums_rows], small_sem.at[LAST_ITEMS])
     for t in range(FIRST_LAST, ITEMS + PER * LAG_D):
         if t < ITEMS:
             for m in range(per_item):
@@ -580,40 +574,23 @@
             total = ring.stage_d(d, LAST_ROWS)
             for m in range(per_item):
                 small[pl.ds(0, PIECE), cols((d - FIRST_LAST) * per_item + m)] = total[m * PIECE:(m + 1) * PIECE]
-            part_copy(d - FIRST_LAST).start()
         if t == FIRST_LAST + 4:
             stats_wait(st, ssem, rsem, ST_LOSS)
             loss = jnp.sum(stats_total(st, ST_LOSS), keepdims=True)
             small[pl.ds(PIECE + 4, 4), :] = jnp.broadcast_to(loss, (4, WIDTH))
-            sums_copy.start()
         if t == FIRST_LAST:
             st[ST_LOSS, 0, pl.ds(0, 1), :] = loss_acc[...]
             stats_send(me, st, ssem, rsem, ST_LOSS)
-    for t in (FIRST_LAST - 2, FIRST_LAST - 1):
-        out_copy(t, dw2_hbm).wait()
-    sums_copy.wait()
-    for k in range(LAST_ITEMS):
-        part_copy(k).wait()
-
-
-def finish_kernel(dw3_in, dw2_in, small_in, dw1, dw2, dw3, gg1, gs1, gg2, gs2, loss, v3, v2, vs, in_sem, out_sem):
-    loads = [pltpu.make_async_copy(small_in, vs, in_sem.at[0])]
-    stores = [pltpu.make_async_copy(vs.at[pl.ds(0, PIECE)], dw1, out_sem.at[0])]
-    for k, (src, mid, dst) in enumerate(((dw3_in, v3, dw3), (dw2_in, v2, dw2))):
-        for part in range(2):
-            rows = pl.ds(part * TILE // 2, TILE // 2)
-            i = 1 + 2 * k + part
-            loads.append(pltpu.make_async_copy(src.at[rows], mid.at[rows], in_sem.at[i]))
-            stores.append(pltpu.make_async_copy(mid.at[rows], dst.at[rows], out_sem.at[i]))
-    for load in loads:
-        load.start()
-    for load, store in zip(loads, stores):
-        load.wait()
+
+
+def finish_kernel(dw3_in, dw2_in, small, dw1, dw2, dw3, gg1, gs1, gg2, gs2, loss, out_sem):
+    stores = [(dw3_in, dw3), (dw2_in, dw2), (small.at[pl.ds(0, PIECE)], dw1)]
+    for k, ref in enumerate((gs2, gg2, gs1, gg1)):
+        stores.append((small.at[pl.ds(PIECE + k, 1), :], ref))
+    stores = [pltpu.make_async_copy(src, dst, out_sem.at[k]) for k, (src, dst) in enumerate(stores)]
+    for store in stores:
         store.start()
-    for k, ref in enumerate((gs2, gg2, gs1, gg1)):
-        stores.append(pltpu.make_async_copy(vs.at[pl.ds(PIECE + k, 1), :], ref, out_sem.at[5 + k]))
-        stores[-1].start()
-    loss[...] = vs[pl.ds(PIECE + 4, 1), pl.ds(0, 1)]
+    loss[...] = small[pl.ds(PIECE + 4, 1), pl.ds(0, 1)]
     for store in stores:
         store.wait()
 
@@ -624,8 +601,8 @@
 DMA = pltpu.SemaphoreType.DMA
 
 
-def params(collective_id):
-    return pltpu.CompilerParams(collective_id=collective_id, has_side_effects=True, vmem_limit_bytes=64_000_000)
+def params(collective_id, limit):
+    return pltpu.CompilerParams(collective_id=collective_id, has_side_effects=True, vmem_limit_bytes=limit)
 
 
 def solution(mesh):
@@ -653,37 +630,34 @@
                 DMA, DMA((2,)), DMA((2, FWD_TILES)), DMA((3, 2, FWD_TILES)), DMA((6 * FWD_TILES,)), DMA((6 * FWD_TILES,)),
                 DMA((6,)),
             ],
-            compiler_params=params(0), name="forward",
+            compiler_params=params(0, 64_000_000), name="forward",
         )(h_a, h_b, w_one, w_two, w_three, g1, b1, g2, b2)
         dw3, dw2, rest = pl.pallas_call(
             main_kernel,
-            out_shape=(weight, weight, sds((small, WIDTH), F32)),
+            out_shape=(pltpu.VMEM((TILE, WIDTH), F32), pltpu.VMEM((TILE, WIDTH), F32), pltpu.VMEM((small, WIDTH), F32)),
             in_specs=[ANY_SPEC] * 15 + [SMEM_SPEC],
-            out_specs=(ANY_SPEC,) * 3,
+            out_specs=(VMEM_SPEC,) * 3,
             scratch_shapes=[
                 pltpu.VMEM((ROWS, WIDTH), BF16), pltpu.VMEM((TILES, ROWS, TILE), F32),
                 pltpu.VMEM((TILES, ROWS, TILE), F32), pltpu.VMEM((CHUNKS, 2, 2, 2, CHUNK, TILE), BF16),
                 pltpu.VMEM((TILE, WIDTH), BF16),
                 pltpu.VMEM((ROWS, WIDTH), BF16), pltpu.VMEM((ROWS, WIDTH), BF16), pltpu.VMEM((ROWS, WIDTH), BF16),
                 pltpu.VMEM((FEAT, ROWS), BF16), pltpu.VMEM((TILE, ROWS), BF16),
-                pltpu.VMEM((2, TILE, WIDTH), BF16), pltpu.VMEM((2, TILE, CHUNK), F32),
+                pltpu.VMEM((2, TILE, WIDTH), BF16),
                 pltpu.VMEM((1, TILE), F32), pltpu.VMEM((ST_LOSS + 1, 8, 4, TILE), F32),
             ] + small_inputs + [
                 pltpu.VMEM((3, 2, FWD_TILES, 1, FWD_TILE), F32),
-                pltpu.VMEM((small, WIDTH), F32), DMA((LAST_ITEMS + 1,)), DMA((7,)), DMA, DMA((2, TILES)), DMA((2,)), DMA((2,)), DMA((2,)), DMA((ST_LOSS + 1,)), DMA((ST_LOSS + 1,)),
+                DMA((7,)), DMA, DMA((2, TILES)), DMA((2,)), DMA((2,)), DMA((ST_LOSS + 1,)), DMA((ST_LOSS + 1,)),
             ] + [DMA((CHUNKS,))] * 6 + RING_SCRATCH,
-            compiler_params=params(1), name="main",
+            compiler_params=params(1, 61_100_000), name="main",
         )(zh, zn, x2, x1, h_a, h_b, w_three, w_two, xh2, xh1, inv, g1, b1, g2, b2, lam_off.reshape(1, 1))
         dw1, dw2, dw3, gg1, gs1, gg2, gs2, loss = pl.pallas_call(
             finish_kernel,
             out_shape=(sds((PIECE, WIDTH), F32), weight, weight, vector, vector, vector, vector, sds((1, 1), F32)),
-            in_specs=[ANY_SPEC] * 3,
+            in_specs=[VMEM_SPEC] * 3,
             out_specs=(ANY_SPEC,) * 7 + (VMEM_SPEC,),
-            scratch_shapes=[
-                pltpu.VMEM((TILE, WIDTH), F32), pltpu.VMEM((TILE, WIDTH), F32), pltpu.VMEM((small, WIDTH), F32),
-                DMA((5,)), DMA((9,)),
-            ],
-            compiler_params=pltpu.CompilerParams(vmem_limit_bytes=66_000_000), name="finish",
+            scratch_shapes=[DMA((7,))],
+            compiler_params=pltpu.CompilerParams(vmem_limit_bytes=16_000_000), name="finish",
         )(dw3, dw2, rest)
         return (loss.reshape(()), dw1, dw2, dw3, gg1.reshape(WIDTH), gs1.reshape(WIDTH),
                 gg2.reshape(WIDTH), gs2.reshape(WIDTH))

time: 329 us -> 326 us (level)
  no operation moved by 1% of the time
where the time goes in v5:
time: 326 us
  Pallas kernels  325 us (100%)
    pallas_call x1, Pallas kernels, local_step(): pl.pallas_call(main_kernel, out_shape=(pltpu.VMEM((TILE, WIDTH), F32), pl...  282 us
    pallas_call x1, Pallas kernels, local_step(): pl.pallas_call(forward_kernel, out_shape=(sds((3, 2, FWD_TILES, 1, FWD_TI...  40.6 us

profile of v5, /device:TPU:0, one launch (start us, length us, event | category | flops | bytes accessed | tf_op | source)
XLA Modules:
  0.0 326.3 jit_solution(15592474195473795864)
XLA Ops:
  1.3 40.6 %forward.1 = (f32[3,2,4,1,512]{4,3,2,1,0:T(1,128)}, bf16[1024,2048]{1,0:T(8,128)(2,1)}, bf16[1024,2048]{1,0:T(8,128)(2,1)}, bf16[1024,2048]{1,0:T(8,128)(2,1)}, ...) custom-call(bf16[512,384]{1,0:T(8,128)(2,1)} %ha_hbm.3, ...), custom_call_target="tpu_custom_call" | custom-call | tf_op jit(solution)/shard_map/forward/pallas_call | solution.py:619
  41.9 281.5 %main.1 = (f32[256,2048]{1,0:T(8,128)S(1)}, f32[256,2048]{1,0:T(8,128)S(1)}, f32[56,2048]{1,0:T(8,128)S(1)}) custom-call(bf16[1024,2048]{1,0:T(8,128)(2,1)} %get-tuple-element.26.zh_hbm, f32[2,4,512,512]{3,2,1,0:T(8,128)} %get-tuple-element.27.zn_hbm, bf16[1024,2048]{1,0:T(8,128)(2,1)} %get-tuple-element.28.x2_hbm, ...), custom_call_target="tpu_custom_call" | custom-call | tf_op jit(solution)/shard_map/main/pallas_call | solution.py:635
  323.4 2.7 finish.1

commit v6 on v5

--- a/solution.py
+++ b/solution.py
@@ -316,7 +316,9 @@
                 z_sem, normed_sem, x_sem, w_sem, ssem, rsem,
                 es, er, fs, fr, hs, hr, *ring_refs):
     me = lax.axis_index("data")
-    z_copy = pltpu.make_async_copy(zh_hbm, z, z_sem)
+    blocks = ((pl.ds(0, VIEW), slice(None)), (pl.ds(VIEW, VIEW), pl.ds(0, TILE)),
+              (pl.ds(VIEW, VIEW), pl.ds(TILE, WIDTH - TILE)))
+    z_copies = [pltpu.make_async_copy(zh_hbm.at[b], z.at[b], z_sem.at[i]) for i, b in enumerate(blocks)]
     x2_copy = pltpu.make_async_copy(x2_hbm, x2, x_sem.at[0])
     x1_copy = pltpu.make_async_copy(x1_hbm, x1, x_sem.at[1])
 
@@ -325,12 +327,14 @@
             src.at[v, q // RATIO, :, cols(q % RATIO)], normed.at[q, pl.ds(v * VIEW, VIEW)], sem.at[v, q])
             for v in range(2) for q in range(TILES)]
 
-    z_copy.start()
+    for copy in z_copies:
+        copy.start()
     barrier_signal(me)
     ring = Ring(me, ITEMS, *ring_refs[:4], ring_refs[4:10], ring_refs[10:])
     core, f, s = ring.core, ring.f, ring.s
     lam_val = lam[0, 0]
-    z_copy.wait()
+    z_copies[0].wait()
+    z_copies[1].wait()
     for copy in normed_copies(zn_hbm, normed_sem):
         copy.start()
     inputs = copies_in((ha_hbm, hb_hbm, g1_hbm, b1_hbm, g2_hbm, b2_hbm, inv_hbm),
@@ -425,6 +429,7 @@
     corr_partial(0)
     barrier_wait()
     corr_send(0)
+    z_copies[2].wait()
     acc[...] = jnp.zeros_like(acc)
     loss_acc[...] = jnp.zeros_like(loss_acc)
     st[:, 0] = jnp.zeros((st.shape[0],) + st.shape[2:], F32)
@@ -647,7 +652,7 @@
                 pltpu.VMEM((1, TILE), F32), pltpu.VMEM((ST_LOSS + 1, 8, 4, TILE), F32),
             ] + small_inputs + [
                 pltpu.VMEM((3, 2, FWD_TILES, 1, FWD_TILE), F32),
-                DMA((7,)), DMA, DMA((2, TILES)), DMA((2,)), DMA((2,)), DMA((ST_LOSS + 1,)), DMA((ST_LOSS + 1,)),
+                DMA((7,)), DMA((3,)), DMA((2, TILES)), DMA((2,)), DMA((2,)), DMA((ST_LOSS + 1,)), DMA((ST_LOSS + 1,)),
             ] + [DMA((CHUNKS,))] * 6 + RING_SCRATCH,
             compiler_params=params(1, 61_100_000), name="main",
         )(zh, zn, x2, x1, h_a, h_b, w_three, w_two, xh2, xh1, inv, g1, b1, g2, b2, lam_off.reshape(1, 1))

time: 326 us -> 326 us (level)
  no operation moved by 1% of the time
where the time goes in v6:
time: 326 us
  Pallas kernels  324 us (99%)
    pallas_call x1, Pallas kernels, local_step(): pl.pallas_call(main_kernel, out_shape=(pltpu.VMEM((TILE, WIDTH), F32), pl...  281 us
    pallas_call x1, Pallas kernels, local_step(): pl.pallas_call(forward_kernel, out_shape=(sds((3, 2, FWD_TILES, 1, FWD_TI...  40.6 us

profile of v6, /device:TPU:0, one launch (start us, length us, event | category | flops | bytes accessed | tf_op | source)
XLA Modules:
  0.0 325.8 jit_solution(6479328247512123346)
XLA Ops:
  1.3 40.6 %forward.1 = (f32[3,2,4,1,512]{4,3,2,1,0:T(1,128)}, bf16[1024,2048]{1,0:T(8,128)(2,1)}, bf16[1024,2048]{1,0:T(8,128)(2,1)}, bf16[1024,2048]{1,0:T(8,128)(2,1)}, ...) custom-call(bf16[512,384]{1,0:T(8,128)(2,1)} %ha_hbm.3, ...), custom_call_target="tpu_custom_call" | custom-call | tf_op jit(solution)/shard_map/forward/pallas_call | solution.py:624
  41.9 281.0 %main.1 = (f32[256,2048]{1,0:T(8,128)S(1)}, f32[256,2048]{1,0:T(8,128)S(1)}, f32[56,2048]{1,0:T(8,128)S(1)}) custom-call(bf16[1024,2048]{1,0:T(8,128)(2,1)} %get-tuple-element.26.zh_hbm, f32[2,4,512,512]{3,2,1,0:T(8,128)} %get-tuple-element.27.zn_hbm, bf16[1024,2048]{1,0:T(8,128)(2,1)} %get-tuple-element.28.x2_hbm, ...), custom_call_target="tpu_custom_call" | custom-call | tf_op jit(solution)/shard_map/main/pallas_call | solution.py:640
  322.9 2.7 finish.1
